TPU v7x, 256 devices: a whole 4x4x8 slice. The times are simulated.
256 devices in a mesh: dp: 256 (over z, y, x, core).
Axes of the slice: x: 4, y: 4, z: 8, core: 2. Of those that a mesh axis runs over, the one named last changes fastest.
Arguments:
- tokens: bfloat16 [262144, 1024], P('dp'), may hold values from -80 to 80
- seg_ids: int32 [256, 1024], P('dp'), may hold values from 0 to 3, as said below
- counts: int32 [256], replicated, may hold values from 1 to 4, as said below
- positives: int32 [1024], P('dp'), may hold values from 0 to 1023, as said below
- w_qkv: bfloat16 [1024, 1536], replicated, may hold values from -0.1875 to 0.1875
- w_out: bfloat16 [512, 1024], replicated, may hold values from -0.25 to 0.25
- ln_gain: float32 [1024], replicated, may hold values from 0.1 to 1.9
- w_proj: bfloat16 [1024, 2048], replicated, may hold values from -0.1875 to 0.1875
Outputs:
- loss: float32 [1024], P('dp')
- grad_pooled: float32 [1024, 1024], P('dp')
Inputs may be any that keep to these rules, and one draw needn't show every extreme that they name: `seg_ids`: within a rank, the ids never fall and every id from 0 to 3 occurs. Rank r's live segments are its slots 0 to counts[r] - 1; the other slots hold padding; some rank has all 4 live. `positives`: a live slot of another rank, as rank times 4 plus slot.
All inputs are finite; a program needn't handle non-finite values.
Results may differ from a plain program's by a relative error of at most 0.008.
Values may be sent and summed in bfloat16 or wider, within the bound.
No kernel may reach another device: no remote copies, remote signals or barrier semaphores. Data moves between devices by JAX's collectives and lax.ppermute only.
A program may use at most 192 MiB of HBM per device.

v0:
```python
import jax
import jax.numpy as jnp
from jax import lax
from jax.sharding import Mesh
from jax.sharding import PartitionSpec as P

HEADS = 8
DP = ("dp_0", "dp_1", "dp_2", "dp_3")


logit_scale = 20.0


def from_everyone(shard, axis):
    copies = jnp.broadcast_to(shard, (lax.axis_size(axis), *shard.shape))
    return lax.all_to_all(copies, axis, split_axis=0, concat_axis=0, tiled=True)


def joined_along(pieces, dim):
    lengths = list(pieces.shape[1:])
    lengths[dim] *= pieces.shape[0]
    return jnp.moveaxis(pieces, 0, dim).reshape(lengths)


def gathered_by_axis(shard, axes, dim):
    far, near = axes
    leading = from_everyone(shard, far)
    pieces = jnp.swapaxes(from_everyone(leading, near), 0, 1)
    return joined_along(pieces.reshape(-1, *shard.shape), dim)


def attend(tok_rows, segment, w_qkv, w_out, ln_gain):
    rows = tok_rows.shape[0]
    width = w_out.shape[0]
    head_dim = width // HEADS
    qkv = jnp.dot(tok_rows, w_qkv, preferred_element_type=jnp.float32).astype(jnp.bfloat16)
    qkv = qkv.reshape(rows, 3, HEADS, head_dim)
    queries_all = qkv[:, 0]
    keys_all = qkv[:, 1]
    values_all = qkv[:, 2]
    block_rows = min(512, rows)
    pieces = []
    for row_begin in range(0, rows, block_rows):
        query_block = queries_all[row_begin : row_begin + block_rows]
        scores = jnp.einsum(
            "qhd,khd->hqk", query_block, keys_all, preferred_element_type=jnp.float32
        )
        scores = scores * head_dim ** (-0.5)
        same = segment[row_begin : row_begin + block_rows, None] == segment[None, :]
        scores = jnp.where(same[None], scores, -1e30)
        row_max = jnp.max(scores, axis=-1, keepdims=True)
        exp_scores = jnp.exp(scores - row_max)
        probs = (exp_scores / jnp.sum(exp_scores, axis=-1, keepdims=True)).astype(jnp.bfloat16)
        context = jnp.einsum("hqk,khd->qhd", probs, values_all, preferred_element_type=jnp.float32)
        pieces.append(context.astype(jnp.bfloat16).reshape(block_rows, width))
    context = jnp.concatenate(pieces, axis=0)
    resid = tok_rows.astype(jnp.float32) + jnp.dot(
        context, w_out, preferred_element_type=jnp.float32
    )
    centre = resid - jnp.mean(resid, axis=-1, keepdims=True)
    variance = jnp.mean(centre * centre, axis=-1, keepdims=True)
    return (centre * lax.rsqrt(variance + 1e-05) * ln_gain).astype(jnp.bfloat16)


def pool_rows(hidden, segment, slots):
    member = jnp.arange(slots, dtype=jnp.int32)[:, None] == segment[None, :]
    sums = jnp.dot(member.astype(jnp.bfloat16), hidden, preferred_element_type=jnp.float32)
    sizes = jnp.sum(member.astype(jnp.float32), axis=1, keepdims=True)
    return (sums / sizes).astype(jnp.bfloat16)


def embed_rows(pooled, w_proj):
    proj = jnp.dot(pooled, w_proj, preferred_element_type=jnp.float32)
    rnorm = lax.rsqrt(jnp.sum(proj * proj, axis=-1, keepdims=True) + 1e-06)
    return (proj * rnorm, rnorm)


def body(tokens, seg_ids, counts, positives, w_qkv, w_out, ln_gain, w_proj):
    my_rank = lax.axis_index(DP)
    devices = lax.axis_size(DP)
    segment = seg_ids[0]
    slots = positives.shape[0]
    all_slots = slots * devices
    hidden = attend(tokens, segment, w_qkv, w_out, ln_gain)
    pooled = pool_rows(hidden, segment, slots)
    unit, rnorm = embed_rows(pooled, w_proj)
    emb = unit.astype(jnp.bfloat16)
    all_pooled = gathered_by_axis(pooled, (("dp_0", "dp_1"), ("dp_2", "dp_3")), 0)
    all_unit, all_rnorm = embed_rows(all_pooled, w_proj)
    all_emb = all_unit.astype(jnp.bfloat16)
    slot_ids = jnp.arange(all_slots, dtype=jnp.int32)
    own_ids = my_rank * slots + jnp.arange(slots, dtype=jnp.int32)
    live_counts = jnp.broadcast_to(counts[:, None], (devices, slots)).reshape(all_slots)
    live = slot_ids % slots < live_counts
    my_count = lax.dynamic_index_in_dim(counts, my_rank, 0, keepdims=False)
    live_query = jnp.arange(slots, dtype=jnp.int32) < my_count
    logits = logit_scale * lax.dot_general(
        emb, all_emb, (((1,), (1,)), ((), ())), preferred_element_type=jnp.float32
    )
    allowed = live[None, :] & (slot_ids[None, :] != own_ids[:, None])
    exp_logits = jnp.where(allowed, jnp.exp(logits), 0.0)
    denominator = jnp.sum(exp_logits, axis=-1)
    target = slot_ids[None, :] == positives[:, None]
    picked = jnp.sum(jnp.where(target, logits, 0.0), axis=-1)
    loss = jnp.where(live_query, jnp.log(denominator) - picked, 0.0)
    weights = jnp.where(
        live_query[:, None], exp_logits / denominator[:, None] - target.astype(jnp.float32), 0.0
    )
    weights = weights.astype(jnp.bfloat16)
    d_query = logit_scale * jnp.dot(weights, all_emb, preferred_element_type=jnp.float32)
    all_denominator, all_targets = (
        gathered_by_axis(denominator, (("dp_0", "dp_1"), ("dp_2", "dp_3")), 0),
        gathered_by_axis(positives.astype(jnp.float32), (("dp_0", "dp_1"), ("dp_2", "dp_3")), 0),
    )
    all_positives = all_targets.astype(jnp.int32)
    column_logits = logit_scale * lax.dot_general(
        all_emb, emb, (((1,), (1,)), ((), ())), preferred_element_type=jnp.float32
    )
    column_allowed = live_query[None, :] & (slot_ids[:, None] != own_ids[None, :])
    column_exp = jnp.where(column_allowed, jnp.exp(column_logits), 0.0)
    column_hits = (all_positives[:, None] == own_ids[None, :]).astype(jnp.float32)
    column_weights = jnp.where(
        live[:, None], column_exp / all_denominator[:, None] - column_hits, 0.0
    )
    column_weights = column_weights.astype(jnp.bfloat16)
    d_key = logit_scale * lax.dot_general(
        column_weights, all_emb, (((0,), (0,)), ((), ())), preferred_element_type=jnp.float32
    )
    d_emb = d_query + d_key
    radial = jnp.sum(d_emb * unit, axis=-1, keepdims=True)
    d_proj = ((d_emb - radial * unit) * rnorm).astype(jnp.bfloat16)
    grad_pooled = lax.dot_general(
        d_proj, w_proj, (((1,), (1,)), ((), ())), preferred_element_type=jnp.float32
    )
    return (loss, grad_pooled)


def solution(mesh):
    finer = Mesh(mesh.devices.reshape(8, 4, 4, 2), ("dp_0", "dp_1", "dp_2", "dp_3"))
    return jax.shard_map(
        body,
        mesh=finer,
        in_specs=(P(DP, None), P(DP, None), P(), P(DP), P(), P(), P(), P()),
        out_specs=(P(DP), P(DP, None)),
        check_vma=False,
    )
```

profile of v0, /device:TPU:1, one launch (start us, length us, event | category | flops | bytes accessed | tf_op | source)
XLA Modules:
  0.0 223.1 jit_solution(16379266633564425066)
XLA Ops:
  2.1 12.0 %all-to-all-start.4 = ((f32[32,1,4]{2,1,0:T(1,128)}), f32[32,1,4]{2,1,0:T(1,128)S(1)}, u32[]{:S(2)}, u32[]{:S(2)}) async-start(f32[32,1,4]{2,1,0:T(1,128)} %broadcast_in_dim.117), calls=%async_computation.4 | async-start | bytes 32768 | tf_op jit(solution)/shard_map/all_to_all | solution.py:16
  14.1 6.4 %convolution_convert_fusion = bf16[1024,1536]{1,0:T(8,128)(2,1)} fusion(bf16[1024,1024]{1,0:T(8,128)(2,1)} %param.8, bf16[1024,1536]{1,0:T(8,128)(2,1)S(1)} %copy-done), kind=kOutput, calls=%fused_computation.23 | convolution fusion | flops 3222798336 | bytes 8388608 | tf_op jit(solution)/shard_map/dot_general | solution.py:36
  20.5 3.2 %copy.29 = bf16[1024,1536]{0,1:T(8,128)(2,1)S(1)} copy(bf16[1024,1536]{1,0:T(8,128)(2,1)} %convolution_convert_fusion) | data formatting | bytes 6291456 | tf_op jit(solution)/shard_map/convert_element_type | solution.py:36
  23.7 8.1 %fusion.28 = f32[8,512,1024]{2,1,0:T(8,128)} fusion(bf16[1024,3,8,64]{0,3,2,1:T(8,128)(2,1)S(1)} %bitcast.52), kind=kOutput, calls=%fused_computation.47 | convolution fusion | flops 536870912 | bytes 18350080 | tf_op jit(solution)/shard_map/qhd,khd->hqk/dot_general | solution.py:45
  31.8 8.1 %fusion.27 = f32[8,512,1024]{2,1,0:T(8,128)} fusion(bf16[1024,3,8,64]{0,3,2,1:T(8,128)(2,1)S(1)} %bitcast.53), kind=kOutput, calls=%fused_computation.46 | convolution fusion | flops 536870912 | bytes 18350080 | tf_op jit(solution)/shard_map/qhd,khd->hqk/dot_general | solution.py:45
  39.9 3.9 %copy.28 = bf16[1024,1024]{0,1:T(8,128)(2,1)} copy(bf16[1024,1024]{1,0:T(8,128)(2,1)} %param.8) | data formatting | bytes 4194304 | tf_op args[0]
  43.8 1.6 broadcast_compare_fusion.1
  45.5 21.6 %fusion.67 = (f32[8,512]{1,0:T(8,128)S(1)}, f32[8,512,1024]{2,1,0:T(8,128)}) fusion(f32[8,512,1024]{2,1,0:T(8,128)} %fusion.28, pred[512,1024]{1,0:T(8,128)(4,1)} %get-tuple-element.4), kind=kOutput, calls=%fused_computation.110 | output fusion | flops 25166848 | bytes 34095104 | tf_op jit(solution)/shard_map/sub | solution.py:52
  67.0 7.9 %fusion.15 = bf16[8,64,512]{2,1,0:T(8,128)(2,1)} fusion(f32[8,512,1024]{2,1,0:T(8,128)} %get-tuple-element.11, f32[8,512]{1,0:T(8,128)S(1)} %get-tuple-element.10, bf16[1024,3,8,64]{0,3,2,1:T(8,128)(2,1)S(1)} %bitcast.54), kind=kOutput, calls=%fused_computation.28 | convolution fusion | flops 545521664 | bytes 18366464 | tf_op jit(solution)/shard_map/hqk,khd->qhd/dot_general | solution.py:54
  75.0 21.7 %fusion.66 = (f32[8,512]{1,0:T(8,128)S(1)}, f32[8,512,1024]{2,1,0:T(8,128)}) fusion(f32[8,512,1024]{2,1,0:T(8,128)} %fusion.27, pred[512,1024]{1,0:T(8,128)(4,1)} %get-tuple-element.5), kind=kOutput, calls=%fused_computation.109 | output fusion | flops 25166848 | bytes 34095104 | tf_op jit(solution)/shard_map/sub | solution.py:52
  96.6 7.4 %fusion.14 = bf16[8,64,512]{2,1,0:T(8,128)(2,1)S(1)} fusion(f32[8,512,1024]{2,1,0:T(8,128)} %get-tuple-element.9, f32[8,512]{1,0:T(8,128)S(1)} %get-tuple-element.8, bf16[1024,3,8,64]{0,3,2,1:T(8,128)(2,1)S(1)} %bitcast.55), kind=kOutput, calls=%fused_computation.27 | convolution fusion | flops 545521664 | bytes 18366464 | tf_op jit(solution)/shard_map/hqk,khd->qhd/dot_general | solution.py:54
  104.1 1.4 fusion.68
  105.6 1.9 copy-done.3
  108.8 5.3 %all-to-all-start.5 = ((f32[8,1,128]{2,1,0:T(1,128)}), f32[8,1,128]{2,1,0:T(1,128)S(1)}, u32[]{:S(2)}, u32[]{:S(2)}) async-start(f32[8,1,128]{2,1,0:T(1,128)} %reshape.179), calls=%async_computation.5 | async-start | bytes 8192 | tf_op jit(solution)/shard_map/all_to_all | solution.py:16
  114.1 2.9 %fusion.23 = bf16[4,1024]{1,0:T(4,128)(2,1)S(1)} fusion(f32[1024,1024]{0,1:T(8,128)} %copy-done.3, f32[1024]{0:T(1024)S(1)} %copy-done.6, f32[1024]{0:T(1024)S(1)} %add_rsqrt_fusion.1, f32[1024]{0:T(1024)S(1)} %broadcast_multiply_fusion, f32[4]{0:T(128)S(1)} %convert_reduce_fusion, s32[1024]{0:T(1024)S(1)} %bitcast.59), kind=kOutput, calls=%fused_computation.38 | convolution fusion | flops 12595200 | bytes 4218896 | tf_op jit(solution)/shard_map/dot_general | solution.py:67
  117.0 1.6 all-to-all-done.5
  118.7 20.6 %all_to_all.38 = bf16[32,4,1024]{2,1,0:T(4,128)(2,1)S(1)} all-to-all(bf16[32,4,1024]{2,1,0:T(4,128)(2,1)S(1)} %broadcast_in_dim.108), channel_id=1, replica_groups=mesh['dp_0'=8,'dp_1'=4,'dp_2'=4,'dp_3'=2] {'dp_0','dp_1'}, dimensions={0} | all-to-all | bytes 524288 | tf_op jit(solution)/shard_map/all_to_all | solution.py:16
  139.3 2.1 broadcast_in_dim.109
  141.3 6.0 %all-to-all-start.1 = ((bf16[8,32,4,1024]{3,2,1,0:T(4,128)(2,1)}), bf16[8,32,4,1024]{3,2,1,0:T(4,128)(2,1)S(1)}, u32[]{:S(2)}, u32[]{:S(2)}) async-start(bf16[8,32,4,1024]{3,2,1,0:T(4,128)(2,1)} %broadcast_in_dim.109), calls=%async_computation.1 | async-start | bytes 4194304 | tf_op jit(solution)/shard_map/all_to_all | solution.py:16
  148.8 3.0 %multiply_reduce_fusion.3 = (f32[4]{0:T(128)S(1)}, f32[4,2048]{1,0:T(4,128)S(1)}) fusion(bf16[4,1024]{1,0:T(4,128)(2,1)S(1)} %fusion.23, bf16[1024,2048]{1,0:T(8,128)(2,1)} %param.15), kind=kOutput, calls=%fused_computation.52 | convolution fusion | flops 16793596 | bytes 4235280 | tf_op jit(solution)/shard_map/dot_general | solution.py:73
  153.3 20.3 %all-to-all-done.1 = bf16[8,32,4,1024]{3,2,1,0:T(4,128)(2,1)S(1)} async-done(((bf16[8,32,4,1024]{3,2,1,0:T(4,128)(2,1)}), bf16[8,32,4,1024]{3,2,1,0:T(4,128)(2,1)S(1)}, u32[]{:S(2)}, u32[]{:S(2)}) %all-to-all-start.1) | async-done | bytes 2097184 | tf_op jit(solution)/shard_map/all_to_all | solution.py:16
  173.5 2.5 %copy.30 = bf16[32,8,4,1024]{3,2,1,0:T(4,128)(2,1)} copy(bf16[32,8,4,1024]{3,2,0,1:T(4,128)(2,1)S(1)} %bitcast.56) | data formatting | bytes 4194304 | tf_op jit(solution)/shard_map/transpose | solution.py:28
  176.0 2.5 %reshape_reshape.4 = bf16[1024,1024]{1,0:T(8,128)(2,1)S(1)} reshape(bf16[32,8,4,1024]{3,2,1,0:T(4,128)(2,1)} %copy.30) | data formatting | bytes 4194304 | tf_op jit(solution)/shard_map/reshape;reshape | solution.py:22
  178.6 6.4 %multiply_reduce_fusion = (f32[1024]{0:T(1024)S(1)}, f32[1024,2048]{1,0:T(8,128)S(1)}) fusion(bf16[1024,1024]{1,0:T(8,128)(2,1)S(1)} %reshape_reshape.4, bf16[1024,2048]{1,0:T(8,128)(2,1)} %param.15), kind=kOutput, calls=%fused_computation.11 | convolution fusion | flops 4299160576 | bytes 14684160 | tf_op jit(solution)/shard_map/dot_general | solution.py:73
  185.6 1.9 copy-done.2
  189.4 3.8 %all-to-all-start.2 = ((f32[32,1,4]{2,1,0:T(1,128)}), f32[32,1,4]{2,1,0:T(1,128)S(1)}, u32[]{:S(2)}, u32[]{:S(2)}) async-start(f32[32,1,4]{2,1,0:T(1,128)} %broadcast_in_dim.115), calls=%async_computation.2 | async-start | bytes 32768 | tf_op jit(solution)/shard_map/all_to_all | solution.py:16
  193.3 2.9 %fusion.38 = f32[4,2048]{1,0:T(4,128)S(1)} fusion(bf16[1024,2048]{1,0:T(8,128)(2,1)} %copy-done.2, f32[4,1024]{1,0:T(4,128)S(1)} %get-tuple-element.18, f32[4]{0:T(128)S(1)} %get-tuple-element.2, s32[4]{0:T(128)S(1)} %copy-done.7, s32[4]{0:T(128)S(1)} %iota_add_fusion, pred[4]{0:T(512)(128)(4,1)S(1)} %iota_compare_fusion.5, pred[1024]{0:T(1024)(128)(4,1)S(1)} %fusion.53), kind=kOutput, calls=%fused_computation.72 | convolution fusion | flops 16814080 | bytes 4244532 | tf_op jit(solution)/shard_map/dot_general | solution.py:110
  196.2 5.7 %all-to-all-done.2 = f32[32,1,4]{2,1,0:T(1,128)S(1)} async-done(((f32[32,1,4]{2,1,0:T(1,128)}), f32[32,1,4]{2,1,0:T(1,128)S(1)}, u32[]{:S(2)}, u32[]{:S(2)}) %all-to-all-start.2) | async-done | bytes 544 | tf_op jit(solution)/shard_map/all_to_all | solution.py:16
  202.6 5.5 %all-to-all-start.3 = ((f32[8,1,128]{2,1,0:T(1,128)}), f32[8,1,128]{2,1,0:T(1,128)S(1)}, u32[]{:S(2)}, u32[]{:S(2)}) async-start(f32[8,1,128]{2,1,0:T(1,128)} %reshape.181), calls=%async_computation.3 | async-start | bytes 8192 | tf_op jit(solution)/shard_map/all_to_all | solution.py:16
  209.2 3.4 %all-to-all-done.3 = f32[8,1,128]{2,1,0:T(1,128)S(1)} async-done(((f32[8,1,128]{2,1,0:T(1,128)}), f32[8,1,128]{2,1,0:T(1,128)S(1)}, u32[]{:S(2)}, u32[]{:S(2)}) %all-to-all-start.3) | async-done | bytes 4128 | tf_op jit(solution)/shard_map/all_to_all | solution.py:16
  213.6 5.5 %multiply_reduce_fusion.2 = (f32[4]{0:T(128)S(1)}, f32[4,2048]{1,0:T(4,128)S(1)}) fusion(f32[4,2048]{1,0:T(4,128)S(1)} %get-tuple-element.17, f32[4]{0:T(128)S(1)} %add_rsqrt_fusion.2, f32[4,2048]{1,0:T(4,128)S(1)} %fusion.38, bf16[1024,2048]{1,0:T(8,128)(2,1)} %copy-done.2, s32[1024]{0:T(1024)S(1)} %convert_element_type.89, f32[1024]{0:T(1024)S(1)} %div.58, ...), kind=kOutput, calls=%fused_computation.51 | convolution fusion | flops 33652732 | bytes 4301876 | tf_op jit(solution)/shard_map/dot_general | solution.py:126
  219.1 4.0 %fusion.29 = f32[4,1024]{1,0:T(4,128)} fusion(bf16[1024,2048]{1,0:T(8,128)(2,1)} %param.15, f32[4,2048]{1,0:T(4,128)S(1)} %get-tuple-element.20, f32[4,2048]{1,0:T(4,128)S(1)} %get-tuple-element.17, f32[4]{0:T(128)S(1)} %get-tuple-element.19, f32[4]{0:T(128)S(1)} %add_rsqrt_fusion.2), kind=kOutput, calls=%fused_computation.55 | convolution fusion | flops 16818176 | bytes 4276256 | tf_op jit(solution)/shard_map/dot_general | solution.py:132
  (58 shorter events, 11.2 us)
Async XLA Ops:
  0.6 13.5 %copy-start = (bf16[1024,1536]{1,0:T(8,128)(2,1)S(1)}, bf16[1024,1536]{1,0:T(8,128)(2,1)}, u32[]{:S(2)}) copy-start(bf16[1024,1536]{1,0:T(8,128)(2,1)} %param.12) | copy-start | bytes 9437188
  2.1 106.0 %all-to-all-start.4 = ((f32[32,1,4]{2,1,0:T(1,128)}), f32[32,1,4]{2,1,0:T(1,128)S(1)}, u32[]{:S(2)}, u32[]{:S(2)}) async-start(f32[32,1,4]{2,1,0:T(1,128)} %broadcast_in_dim.117), calls=%async_computation.4 | async-start | bytes 32768 | tf_op jit(solution)/shard_map/all_to_all | solution.py:16
  39.9 4.0 %copy-start.5 = (s32[1,1024]{1,0:T(1,128)S(1)}, s32[1,1024]{1,0:T(1,128)}, u32[]{:S(2)}) copy-start(s32[1,1024]{1,0:T(1,128)} %param.9) | copy-start | bytes 12292
  96.6 7.4 %copy-start.4 = (bf16[1024,1024]{0,1:T(8,128)(2,1)S(1)}, bf16[1024,1024]{0,1:T(8,128)(2,1)}, u32[]{:S(2)}) copy-start(bf16[1024,1024]{0,1:T(8,128)(2,1)} %copy.28) | copy-start | bytes 6291460
  96.6 7.4 %copy-start.9 = (bf16[512,1024]{1,0:T(8,128)(2,1)S(1)}, bf16[512,1024]{1,0:T(8,128)(2,1)}, u32[]{:S(2)}) copy-start(bf16[512,1024]{1,0:T(8,128)(2,1)} %param.13) | copy-start | bytes 3145732
  96.6 7.4 %copy-start.10 = (bf16[8,64,512]{2,1,0:T(8,128)(2,1)S(1)}, bf16[8,64,512]{2,1,0:T(8,128)(2,1)}, u32[]{:S(2)}) copy-start(bf16[8,64,512]{2,1,0:T(8,128)(2,1)} %fusion.15) | copy-start | bytes 1572868
  105.5 1.9 copy-start.3
  105.5 8.6 %copy-start.6 = (f32[1024]{0:T(1024)S(1)}, f32[1024]{0:T(1024)}, u32[]{:S(2)}) copy-start(f32[1024]{0:T(1024)} %param.14) | copy-start | bytes 12292
  108.8 9.8 %all-to-all-start.5 = ((f32[8,1,128]{2,1,0:T(1,128)}), f32[8,1,128]{2,1,0:T(1,128)S(1)}, u32[]{:S(2)}, u32[]{:S(2)}) async-start(f32[8,1,128]{2,1,0:T(1,128)} %reshape.179), calls=%async_computation.5 | async-start | bytes 8192 | tf_op jit(solution)/shard_map/all_to_all | solution.py:16
  117.0 30.3 %copy-start.8 = (s32[256]{0:T(256)S(1)}, s32[256]{0:T(256)}, u32[]{:S(2)}) copy-start(s32[256]{0:T(256)} %param.10) | copy-start | bytes 3076
  141.3 32.2 %all-to-all-start.1 = ((bf16[8,32,4,1024]{3,2,1,0:T(4,128)(2,1)}), bf16[8,32,4,1024]{3,2,1,0:T(4,128)(2,1)S(1)}, u32[]{:S(2)}, u32[]{:S(2)}) async-start(bf16[8,32,4,1024]{3,2,1,0:T(4,128)(2,1)} %broadcast_in_dim.109), calls=%async_computation.1 | async-start | bytes 4194304 | tf_op jit(solution)/shard_map/all_to_all | solution.py:16
  185.0 2.5 %copy-start.7 = (s32[4]{0:T(128)S(1)}, s32[4]{0:T(128)}, u32[]{:S(2)}) copy-start(s32[4]{0:T(128)} %param.11) | copy-start | bytes 52
  185.6 1.9 copy-start.2
  189.4 12.4 %all-to-all-start.2 = ((f32[32,1,4]{2,1,0:T(1,128)}), f32[32,1,4]{2,1,0:T(1,128)S(1)}, u32[]{:S(2)}, u32[]{:S(2)}) async-start(f32[32,1,4]{2,1,0:T(1,128)} %broadcast_in_dim.115), calls=%async_computation.2 | async-start | bytes 32768 | tf_op jit(solution)/shard_map/all_to_all | solution.py:16
  202.6 10.0 %all-to-all-start.3 = ((f32[8,1,128]{2,1,0:T(1,128)}), f32[8,1,128]{2,1,0:T(1,128)S(1)}, u32[]{:S(2)}, u32[]{:S(2)}) async-start(f32[8,1,128]{2,1,0:T(1,128)} %reshape.181), calls=%async_computation.3 | async-start | bytes 8192 | tf_op jit(solution)/shard_map/all_to_all | solution.py:16
  213.6 9.5 %copy-start.1 = (bf16[1024,1536]{1,0:T(8,128)(2,1)S(1)}, bf16[1024,1536]{1,0:T(8,128)(2,1)}, u32[]{:S(2)}) copy-start(bf16[1024,1536]{1,0:T(8,128)(2,1)} %param.12) | copy-start | bytes 9437188
where the time goes:
time: 224 us; the launch traced here: 223 us
  matrix products  65.3 us (29%)
  other arithmetic  49.8 us (22%)
  starting transfers between devices  32.5 us (15%)
  waiting for transfers between devices  31 us (14%)
  local copies, waits for them, and re-layouts  23 us (10%)
  blocking collectives  20.6 us (9%)
    sub x2, other arithmetic, attend(): exp_scores = jnp.exp(scores - row_max)  43.2 us
    all_to_all x5, starting transfers between devices, from_everyone(): return lax.all_to_all(copies, axis, split_axis=0, concat_axis=0, tiled=True)  32.5 us
    all_to_all x5, waiting for transfers between devices, from_everyone(): return lax.all_to_all(copies, axis, split_axis=0, concat_axis=0, tiled=True)  31 us
    all_to_all x1, blocking collectives, from_everyone(): return lax.all_to_all(copies, axis, split_axis=0, concat_axis=0, tiled=True)  20.6 us
    dot_general x2, matrix products, attend(): jnp.einsum('qhd,khd->hqk', query_block, keys_all, preferred_element_type=...  16.2 us
    dot_general x2, matrix products, attend(): jnp.einsum('hqk,khd->qhd', probs, values_all, preferred_element_type=jnp....  15.3 us
    dot_general x2, matrix products, embed_rows(): proj = jnp.dot(pooled, w_proj, preferred_element_type=jnp.float32)  9.4 us
    unnamed x29, local copies, waits for them, and re-layouts  9.36 us
  transfers between devices with their start and end apart: 5, of which 4 were waited for; matrix products, arithmetic and copies ran while one was open for 47% of the time, Pallas kernels for 0%

commit v1 on v0

v1 whole, which is shorter than its diff:
```python
import functools
import math

import jax
import jax.numpy as jnp
from jax import lax
from jax.experimental import pallas as pl
from jax.experimental.pallas import tpu as pltpu
from jax.sharding import Mesh
from jax.sharding import PartitionSpec as P

AXES = ("dp_0", "dp_1", "dp_2", "dp_3")
HEADS = 8
HEAD_DIM = 64
PAIRS = HEADS // 2
LOG2E = math.log2(math.e)
LOGIT_SCALE = 20.0
META = 128
FAR = -1e30
BF16 = jnp.bfloat16
F32 = jnp.float32
VMEM_LIMIT = 60 * 1024 * 1024


def dot(a, b):
    return lax.dot_general(a, b, (((1,), (0,)), ((), ())), preferred_element_type=F32)


def dot_nt(a, b):
    return lax.dot_general(a, b, (((1,), (1,)), ((), ())), preferred_element_type=F32)


def rank_of():
    z, y, x, core = (lax.axis_index(a) for a in AXES)
    return ((z * 4 + y) * 4 + x) * 2 + core


def pool_kernel(
    seg_ref,
    counts_ref,
    positives_ref,
    x_hbm,
    wqkv_hbm,
    wout_hbm,
    gain_ref,
    out_ref,
    x_ref,
    wqkv_ref,
    wout_ref,
    q_ref,
    k_ref,
    v_ref,
    ctx_ref,
    sums_ref,
    sems,
    *,
    copies,
    tile,
):
    rows, width = x_ref.shape
    slots = out_ref.shape[1]
    hidden = HEADS * HEAD_DIM
    chunk = 256
    chunks = 3 * hidden // chunk

    x_copy = pltpu.make_async_copy(x_hbm, x_ref, sems.at[0])
    x_copy.start()
    w_copies = []
    for c in range(chunks):
        cols = slice(c * chunk, (c + 1) * chunk)
        w_copies.append(
            pltpu.make_async_copy(wqkv_hbm.at[:, cols], wqkv_ref.at[:, cols], sems.at[1 + c])
        )
        w_copies[-1].start()
    wout_copy = pltpu.make_async_copy(wout_hbm, wout_ref, sems.at[1 + chunks])
    wout_copy.start()

    seg = seg_ref[...]
    begins = [jnp.int32(0)]
    for s in range(1, slots):
        begins.append(jnp.sum((seg < s).astype(F32)).astype(jnp.int32))
    begins.append(jnp.int32(rows))

    row_id = lax.broadcasted_iota(jnp.int32, (rows, 2 * HEAD_DIM), 0)
    lane = lax.broadcasted_iota(jnp.int32, (rows, 2 * HEAD_DIM), 1)
    of_row = jnp.zeros((rows, 2 * HEAD_DIM), jnp.int32)
    for s in range(1, slots):
        of_row += (row_id >= begins[s]).astype(jnp.int32)
    feature = lane % HEAD_DIM
    mine = feature == of_row
    q_mark = jnp.where(mine, 1.0, 0.0).astype(BF16)
    k_mark = jnp.where(mine | (feature >= slots), 0.0, FAR).astype(BF16)
    first_half = lane < HEAD_DIM

    x_copy.wait()
    for c in range(chunks):
        w_copies[c].wait()
        kind, place = divmod(c * chunk, hidden)
        part = dot(x_ref[...], wqkv_ref[:, c * chunk : (c + 1) * chunk])
        if kind == 0:
            part = part * (LOG2E * HEAD_DIM**-0.5)
        part = part.astype(BF16)
        for p in range(chunk // (2 * HEAD_DIM)):
            pair = part[:, p * 2 * HEAD_DIM : (p + 1) * 2 * HEAD_DIM]
            head = place // HEAD_DIM + 2 * p
            if kind == 0:
                q_ref[head] = jnp.where(first_half, pair, q_mark)
                q_ref[head + 1] = jnp.where(first_half, q_mark, pair)
            elif kind == 1:
                k_ref[head] = jnp.where(first_half, pair, k_mark)
                k_ref[head + 1] = jnp.where(first_half, k_mark, pair)
            else:
                one = jnp.ones_like(pair)
                v_ref[head] = jnp.where(first_half, pair, one)
                v_ref[head + 1] = jnp.where(first_half, one, pair)

    wout_copy.wait()
    sums_ref[...] = jnp.zeros_like(sums_ref)
    half = lax.broadcasted_iota(jnp.int32, (tile, 2 * HEAD_DIM), 1) < HEAD_DIM
    key_tile = 128
    key_tiles = rows // key_tile
    widths = [w for w in (3, 4, 5, 6, 8) if w <= key_tiles]

    def one_tile(t, carry):
        r0 = pl.multiple_of(t * tile, tile)
        low = jnp.int32(0)
        high = jnp.int32(rows)
        for s in range(1, slots):
            low = jnp.where(begins[s] <= r0, begins[s], low)
        for s in range(slots - 1, 0, -1):
            high = jnp.where(begins[s] >= r0 + tile, begins[s], high)
        k0 = low // key_tile
        need = (high + key_tile - 1) // key_tile - k0

        for i, w in enumerate(widths):
            above = widths[i - 1] if i else 0

            @pl.when((need > above) & (need <= w))
            def _():
                start = pl.multiple_of(jnp.minimum(k0, key_tiles - w) * key_tile, key_tile)
                for p in range(PAIRS):
                    outs = []
                    for h in (2 * p, 2 * p + 1):
                        q = q_ref[h, pl.ds(r0, tile), :]
                        k = k_ref[h, pl.ds(start, w * key_tile), :]
                        v = v_ref[h, pl.ds(start, w * key_tile), :]
                        s = dot_nt(q, k)
                        e = jnp.exp2(s - jnp.max(s, axis=1, keepdims=True)).astype(BF16)
                        outs.append(dot(e, v))
                    top = jnp.where(half, outs[0], outs[1])
                    bottom = jnp.where(half, outs[1], outs[0])
                    bottom = pltpu.roll(bottom, HEAD_DIM, 1)
                    ctx_ref[:, p * 2 * HEAD_DIM : (p + 1) * 2 * HEAD_DIM] = (top / bottom).astype(BF16)

        resid = x_ref[pl.ds(r0, tile), :].astype(F32) + dot(ctx_ref[...], wout_ref[...])
        centre = resid - jnp.mean(resid, axis=1, keepdims=True)
        variance = jnp.mean(centre * centre, axis=1, keepdims=True)
        out = (centre * lax.rsqrt(variance + 1e-05) * gain_ref[...]).astype(BF16)
        slot = lax.broadcasted_iota(jnp.int32, (16, tile), 0)
        token = lax.broadcasted_iota(jnp.int32, (16, tile), 1) + r0
        member = jnp.zeros((16, tile), jnp.bool_)
        for s in range(slots):
            member |= (slot == s) & (token >= begins[s]) & (token < begins[s + 1])
        sums_ref[...] += dot(jnp.where(member, 1.0, 0.0).astype(BF16), out)
        return carry

    lax.fori_loop(0, rows // tile, one_tile, 0)

    slot_col = lax.broadcasted_iota(jnp.int32, (slots, 1), 0)
    sizes = jnp.ones((slots, 1), F32)
    for s in range(slots):
        sizes = jnp.where(slot_col == s, (begins[s + 1] - begins[s]).astype(F32), sizes)
    pooled = (sums_ref[0:slots, :] / sizes).astype(BF16)

    rank = rank_of()
    count = counts_ref[rank]
    line = lax.broadcasted_iota(jnp.int32, (slots, META), 0)
    col = lax.broadcasted_iota(jnp.int32, (slots, META), 1)
    positive = jnp.zeros((slots, META), jnp.int32)
    for s in range(slots):
        positive = jnp.where(line == s, positives_ref[s], positive)
    own = rank * slots + line
    meta = jnp.where(col == 0, positive >> 5, 0)
    meta = jnp.where(col == 1, positive & 31, meta)
    meta = jnp.where(col == 2, (line < count).astype(jnp.int32), meta)
    meta = jnp.where(col == 3, own >> 5, meta)
    meta = jnp.where(col == 4, own & 31, meta)
    meta = meta.astype(F32).astype(BF16)
    for i in range(copies):
        out_ref[i, :, 0:width] = pooled
        out_ref[i, :, width:] = meta


def pooled_rows(tokens, seg_ids, counts, positives, w_qkv, w_out, ln_gain, copies):
    rows, width = tokens.shape
    slots = positives.shape[0]
    hidden = w_out.shape[0]
    tile = 256
    any_spec = pl.BlockSpec(memory_space=pl.ANY)
    vmem = pl.BlockSpec(memory_space=pltpu.VMEM)
    smem = pl.BlockSpec(memory_space=pltpu.SMEM)
    return pl.pallas_call(
        functools.partial(pool_kernel, copies=copies, tile=tile),
        out_shape=jax.ShapeDtypeStruct((copies, slots, width + META), BF16),
        in_specs=[vmem, smem, smem, any_spec, any_spec, any_spec, vmem],
        out_specs=vmem,
        scratch_shapes=[
            pltpu.VMEM((rows, width), BF16),
            pltpu.VMEM((width, 3 * hidden), BF16),
            pltpu.VMEM((hidden, width), BF16),
            pltpu.VMEM((HEADS, rows, 2 * HEAD_DIM), BF16),
            pltpu.VMEM((HEADS, rows, 2 * HEAD_DIM), BF16),
            pltpu.VMEM((HEADS, rows, 2 * HEAD_DIM), BF16),
            pltpu.VMEM((tile, hidden), BF16),
            pltpu.VMEM((16, width), F32),
            pltpu.SemaphoreType.DMA((8,)),
        ],
        compiler_params=pltpu.CompilerParams(vmem_limit_bytes=VMEM_LIMIT),
        cost_estimate=pl.CostEstimate(
            flops=2 * rows * width * 4 * hidden + 4 * rows * rows * hidden,
            bytes_accessed=2 * (rows * width + 4 * width * hidden),
            transcendentals=HEADS * rows * rows // 2,
        ),
        name="pool",
    )(seg_ids, counts, positives, tokens, w_qkv, w_out, ln_gain.reshape(1, width))


def loss_kernel(
    mine_ref,
    other_ref,
    gram_ref,
    loss_ref,
    grad_ref,
    left_ref,
    right_ref,
    logit_ref,
    norm_ref,
):
    total, width = left_ref.shape
    part = total // 2
    slots = grad_ref.shape[0]
    block = 256
    gram = gram_ref[...]

    for b in range(total // block):
        ref = mine_ref if b * block < part else other_ref
        begin = b * block % part
        rows = slice(b * block, (b + 1) * block)
        pooled = ref[begin : begin + block, 0:width]
        through = dot(pooled, gram)
        wide = pooled.astype(F32)
        square = jnp.sum(through * wide, axis=1, keepdims=True)
        rnorm = lax.rsqrt(jnp.maximum(square, 0.0) + 1e-06)
        left_ref[rows, :] = (through * (rnorm * (LOGIT_SCALE * LOG2E))).astype(BF16)
        right_ref[rows, :] = (wide * rnorm).astype(BF16)
        norm_ref[rows, :] = jnp.broadcast_to(rnorm, (block, 128))

    meta = jnp.concatenate([mine_ref[:, width:], other_ref[:, width:]], axis=0)
    pick = lax.broadcasted_iota(jnp.int32, (16, META), 0) == lax.broadcasted_iota(
        jnp.int32, (16, META), 1
    )
    lines = dot_nt(pick.astype(F32).astype(BF16), meta)
    spread = (lax.broadcasted_iota(jnp.int32, (META, 128), 0) == 2).astype(F32).astype(BF16)
    live_col = dot(meta, spread)

    right = right_ref[...]
    sums = jnp.zeros((8, total), F32)
    for b in range(total // block):
        rows = slice(b * block, (b + 1) * block)
        logit = dot_nt(left_ref[rows, :], right)
        logit_ref[rows, :] = logit
        live = live_col[rows, :]
        pieces = []
        for c in range(total // 128):
            term = jnp.exp2(logit[:, c * 128 : (c + 1) * 128]) * live
            if b * block <= c * 128 < (b + 1) * block:
                row = lax.broadcasted_iota(jnp.int32, (block, 128), 0) + b * block
                col = lax.broadcasted_iota(jnp.int32, (block, 128), 1) + c * 128
                term = jnp.where(row == col, 0.0, term)
            pieces.append(jnp.sum(term.reshape(block // 8, 8, 128), axis=0))
        sums = sums + jnp.concatenate(pieces, axis=1)
    denominator_line = jnp.sum(sums, axis=0, keepdims=True)

    z, y, x, _ = (lax.axis_index(a) for a in AXES)
    begin = ((y * 4 + x) * 8 + z) * slots
    base = pl.multiple_of(begin // 16 * 16, 16)
    within = begin - base
    own_meta = mine_ref[pl.ds(base, 16), width:].astype(F32)
    own_positive = own_meta[:, 0:1] * 32.0 + own_meta[:, 1:2]
    own_live = own_meta[:, 2:3] > 0.5
    own_slot = own_meta[:, 3:4] * 32.0 + own_meta[:, 4:5]
    positive_line = lines[0:1, :] * 32.0 + lines[1:2, :]
    live_line = lines[2:3, :] > 0.5
    slot_line = lines[3:4, :] * 32.0 + lines[4:5, :]

    logit = logit_ref[pl.ds(base, 16), :]
    same = slot_line == own_slot
    raw = jnp.where(same, 0.0, jnp.exp2(logit))
    as_query = jnp.where(live_line, raw, 0.0)
    denominator = jnp.sum(as_query, axis=1, keepdims=True)
    target = slot_line == own_positive
    picked = jnp.sum(jnp.where(target, logit, 0.0), axis=1, keepdims=True) * (1.0 / LOG2E)
    loss = jnp.where(own_live, jnp.log(denominator) - picked, 0.0)
    for s in range(slots):
        row = lax.broadcasted_iota(jnp.int32, (16, 1), 0)
        loss_ref[s] = jnp.sum(jnp.where(row == within + s, loss, 0.0))
    query_weights = jnp.where(own_live, as_query / denominator - target.astype(F32), 0.0)
    hits = (positive_line == own_slot).astype(F32)
    key_weights = jnp.where(
        live_line, jnp.where(own_live, raw, 0.0) / denominator_line - hits, 0.0
    )
    weights = (query_weights + key_weights).astype(BF16)
    mix = dot(weights, right)
    image = dot(mix.astype(BF16), gram) * LOGIT_SCALE
    unit_image = left_ref[pl.ds(base, 16), :].astype(F32) * (1.0 / (LOGIT_SCALE * LOG2E))
    radial = LOGIT_SCALE * jnp.sum(mix * unit_image, axis=1, keepdims=True)
    rnorm = norm_ref[pl.ds(base, 16), 0:1]
    grad = (image - radial * unit_image) * rnorm
    out = grad[0:slots]
    for i in range(1, 16 // slots):
        out = jnp.where(within == i * slots, grad[i * slots : (i + 1) * slots], out)
    grad_ref[...] = out


def loss_and_grad(mine, other, gram, slots):
    part, padded = mine.shape
    width = padded - META
    total = 2 * part
    vmem = pl.BlockSpec(memory_space=pltpu.VMEM)
    return pl.pallas_call(
        loss_kernel,
        out_shape=(
            jax.ShapeDtypeStruct((slots,), F32),
            jax.ShapeDtypeStruct((slots, width), F32),
        ),
        in_specs=[vmem, vmem, vmem],
        out_specs=(pl.BlockSpec(memory_space=pltpu.SMEM), vmem),
        scratch_shapes=[
            pltpu.VMEM((total, width), BF16),
            pltpu.VMEM((total, width), BF16),
            pltpu.VMEM((total, total), F32),
            pltpu.VMEM((total, 128), F32),
        ],
        compiler_params=pltpu.CompilerParams(vmem_limit_bytes=VMEM_LIMIT),
        cost_estimate=pl.CostEstimate(
            flops=4 * total * total * width,
            bytes_accessed=4 * total * width,
            transcendentals=total * total,
        ),
        name="loss",
    )(mine, other, gram)


def body(tokens, seg_ids, counts, positives, w_qkv, w_out, ln_gain, w_proj):
    slots = positives.shape[0]
    z_size = lax.axis_size("dp_0")
    plane = ("dp_1", "dp_2")
    plane_size = lax.axis_size(plane)
    packed = pooled_rows(tokens, seg_ids, counts, positives, w_qkv, w_out, ln_gain, z_size)
    padded = packed.shape[-1]
    line = lax.all_to_all(packed, "dp_0", split_axis=0, concat_axis=0, tiled=True)
    line = line.reshape(z_size * slots, padded)
    copies = jnp.broadcast_to(line, (plane_size, *line.shape))
    mine = lax.all_to_all(copies, plane, split_axis=0, concat_axis=0, tiled=True)
    mine = mine.reshape(plane_size * z_size * slots, padded)
    other = lax.ppermute(mine, "dp_3", [(0, 1), (1, 0)])
    gram = lax.dot_general(
        w_proj, w_proj, (((1,), (1,)), ((), ())), preferred_element_type=F32
    ).astype(BF16)
    return loss_and_grad(mine, other, gram, slots)


def solution(mesh):
    finer = Mesh(mesh.devices.reshape(8, 4, 4, 2), AXES)
    return jax.shard_map(
        body,
        mesh=finer,
        in_specs=(P(AXES, None), P(AXES, None), P(), P(AXES), P(), P(), P(), P()),
        out_specs=(P(AXES), P(AXES, None)),
        check_vma=False,
    )
```

time: 224 us -> 88.7 us (0.40)
  matrix products: 65.3 us -> 9.33 us
  other arithmetic: 49.8 us -> 0 us
  Pallas kernels: 0 us -> 33.1 us
  waiting for transfers between devices: 31 us -> 0.01 us
  starting transfers between devices: 32.5 us -> 2.73 us
  local copies, waits for them, and re-layouts: 23 us -> 1.16 us
  blocking collectives: 20.6 us -> 41.9 us
    dot_general x13 -> x1, matrix products: 65.3 us -> 9.33 us  [body(): lax.dot_general(w_proj, w_proj, (((1,), (1,)), ((), ())), preferred_eleme...]
    sub x2 -> x0, other arithmetic: 43.2 us -> none  [attend(): exp_scores = jnp.exp(scores - row_max)]
    pallas_call x0 -> x2, Pallas kernels: none -> 33.1 us  [the longest x1 24.5 us: pooled_rows(): pl.pallas_call(functools.partial(pool_kernel, copies=copies, tile=tile),...]
    all_to_all x5 -> x0, starting transfers between devices: 32.5 us -> none  [from_everyone(): return lax.all_to_all(copies, axis, split_axis=0, concat_axis=0, tiled=True)]
    all_to_all x5 -> x0, waiting for transfers between devices: 31 us -> none  [from_everyone(): return lax.all_to_all(copies, axis, split_axis=0, concat_axis=0, tiled=True)]
    all_to_all x1 -> x2, blocking collectives: 20.6 us -> 41.9 us  [the longest x1 25.3 us: body(): lax.all_to_all(copies, plane, split_axis=0, concat_axis=0, tiled=True)]
    unnamed x29 -> x4, local copies, waits for them, and re-layouts: 9.36 us -> 1.05 us
    convert_element_type x3 -> x0, local copies, waits for them, and re-layouts: 3.44 us -> none  [the longest x1 3.18 us: attend(): jnp.dot(tok_rows, w_qkv, preferred_element_type=jnp.float32)]
  transfers between devices with their start and end apart: 5 -> 1, of which waited for: 4 -> 0; matrix products, arithmetic and copies ran while one was open for 47% -> 10% of each run, Pallas kernels for 0% -> 0%
where the time goes in v1:
time: 88.7 us; the launch traced here: 89.1 us
  blocking collectives  41.9 us (47%)
  Pallas kernels  33.1 us (37%)
  matrix products  9.33 us (11%)
  starting transfers between devices  2.73 us (3%)
  local copies, waits for them, and re-layouts  1.16 us (1%)
    all_to_all x1, blocking collectives, body(): lax.all_to_all(copies, plane, split_axis=0, concat_axis=0, tiled=True)  25.3 us
    pallas_call x1, Pallas kernels, pooled_rows(): pl.pallas_call(functools.partial(pool_kernel, copies=copies, tile=tile),...  24.5 us
    all_to_all x1, blocking collectives, body(): lax.all_to_all(packed, 'dp_0', split_axis=0, concat_axis=0, tiled=True)  16.6 us
    dot_general x1, matrix products, body(): lax.dot_general(w_proj, w_proj, (((1,), (1,)), ((), ())), preferred_eleme...  9.33 us
    pallas_call x1, Pallas kernels, loss_and_grad(): pl.pallas_call(loss_kernel, out_shape=(jax.ShapeDtypeStruct((slots,), F32...  8.61 us
    ppermute x1, starting transfers between devices, body(): other = lax.ppermute(mine, 'dp_3', [(0, 1), (1, 0)])  2.73 us
  transfers between devices with their start and end apart: 1, of which 0 were waited for; matrix products, arithmetic and copies ran while one was open for 10% of the time, Pallas kernels for 0%

profile of v1, /device:TPU:1, one launch (start us, length us, event | category | flops | bytes accessed | tf_op | source)
XLA Modules:
  0.0 89.1 jit_solution(16815506786121519924)
XLA Ops:
  0.6 24.5 %pool.1 = bf16[8,4,1152]{2,1,0:T(4,128)(2,1)} custom-call(s32[1,1024]{1,0:T(1,128)} %seg_ref.1, s32[256]{0:T(256)} %counts_ref.1, s32[4]{0:T(128)} %positives_ref.1, bf16[1024,1024]{1,0:T(8,128)(2,1)} %x_hbm.1, bf16[1024,1536]{1,0:T(8,128)(2,1)} %wqkv_hbm.1, bf16[512,1024]{1,0:T(8,128)(2,1)} %wout_hbm.1, f32[1,1024]{1,0:T(1,128)} %bitcast.6), custom_call_target="tpu_custom_call" | custom-call | flops 6442450944 | bytes 6291456 | tf_op jit(solution)/shard_map/pool/pallas_call | solution.py:202
  25.1 16.6 %all_to_all.10 = bf16[8,4,1152]{2,1,0:T(4,128)(2,1)S(1)} all-to-all(bf16[8,4,1152]{2,1,0:T(4,128)(2,1)} %pool.1), channel_id=1, replica_groups=mesh['dp_0'=8,'dp_1'=4,'dp_2'=4,'dp_3'=2] {'dp_0'}, dimensions={0} | all-to-all | bytes 147456 | tf_op jit(solution)/shard_map/all_to_all | solution.py:361
  41.8 0.1 broadcast_in_dim.3
  41.9 25.3 %all_to_all.11 = bf16[16,32,1152]{2,1,0:T(8,128)(2,1)S(1)} all-to-all(bf16[16,32,1152]{2,1,0:T(8,128)(2,1)S(1)} %broadcast_in_dim.3), channel_id=1, replica_groups=mesh['dp_0'=8,'dp_1'=4,'dp_2'=4,'dp_3'=2] {'dp_1','dp_2'}, dimensions={0} | all-to-all | bytes 2359296 | tf_op jit(solution)/shard_map/all_to_all | solution.py:364
  67.2 0.0 copy-start
  67.2 2.7 %collective-permute-start = (bf16[512,1152]{1,0:T(8,128)(2,1)S(1)}, bf16[512,1152]{1,0:T(8,128)(2,1)S(1)}, u32[]{:S(2)}, u32[]{:S(2)}) collective-permute-start(bf16[512,1152]{1,0:T(8,128)(2,1)S(1)} %bitcast.4), channel_id=1, source_target_pairs={{0,1},{1,0},{2,3},{3,2},{4,5},{5,4},{6,7},{7,6},{8,9},{9,8},{10,11... | collective-permute-start | bytes 3538952 | tf_op jit(solution)/shard_map/ppermute | solution.py:366
  69.9 9.3 %convolution_convert_fusion.gram_ref = bf16[1024,1024]{1,0:T(8,128)(2,1)} fusion(bf16[1024,2048]{1,0:T(8,128)(2,1)} %param.15), kind=kOutput, calls=%fused_computation | convolution fusion | flops 4296015872 | bytes 6291456 | tf_op jit(solution)/shard_map/dot_general | solution.py:367
  79.2 0.0 copy-done
  79.2 0.0 collective-permute-done.other_ref
  79.2 0.0 copy-start.1
  79.2 1.0 %copy-done.1 = bf16[512,1152]{1,0:T(8,128)(2,1)} copy-done((bf16[512,1152]{1,0:T(8,128)(2,1)}, bf16[512,1152]{1,0:T(8,128)(2,1)S(1)}, u32[]{:S(2)}) %copy-start.1) | copy-done | bytes 1179672
  80.3 8.6 %loss.1 = (f32[4]{0:T(128)}, f32[4,1024]{1,0:T(4,128)}) custom-call(bf16[512,1152]{1,0:T(8,128)(2,1)} %bitcast.5, bf16[512,1152]{1,0:T(8,128)(2,1)} %copy-done.1, bf16[1024,1024]{1,0:T(8,128)(2,1)} %convolution_convert_fusion.gram_ref), custom_call_target="tpu_custom_call" | custom-call | flops 4294967296 | bytes 4194304 | tf_op jit(solution)/shard_map/loss/pallas_call | solution.py:330
  (1 shorter events, 0.0 us)
Async XLA Ops:
  67.2 12.1 %copy-start = (bf16[16,32,1152]{2,1,0:T(8,128)(2,1)}, bf16[16,32,1152]{2,1,0:T(8,128)(2,1)S(1)}, u32[]{:S(2)}) copy-start(bf16[16,32,1152]{2,1,0:T(8,128)(2,1)S(1)} %all_to_all.11) | copy-start | bytes 3538948
  67.2 12.1 %collective-permute-start = (bf16[512,1152]{1,0:T(8,128)(2,1)S(1)}, bf16[512,1152]{1,0:T(8,128)(2,1)S(1)}, u32[]{:S(2)}, u32[]{:S(2)}) collective-permute-start(bf16[512,1152]{1,0:T(8,128)(2,1)S(1)} %bitcast.4), channel_id=1, source_target_pairs={{0,1},{1,0},{2,3},{3,2},{4,5},{5,4},{6,7},{7,6},{8,9},{9,8},{10,11... | collective-permute-start | bytes 3538952 | tf_op jit(solution)/shard_map/ppermute | solution.py:366
  79.2 1.0 %copy-start.1 = (bf16[512,1152]{1,0:T(8,128)(2,1)}, bf16[512,1152]{1,0:T(8,128)(2,1)S(1)}, u32[]{:S(2)}) copy-start(bf16[512,1152]{1,0:T(8,128)(2,1)S(1)} %collective-permute-done.other_ref) | copy-start | bytes 3538948

commit v2 on v1

--- a/solution.py
+++ b/solution.py
@@ -19,7 +19,8 @@
 FAR = -1e30
 BF16 = jnp.bfloat16
 F32 = jnp.float32
-VMEM_LIMIT = 60 * 1024 * 1024
+POOL_VMEM = 60 * 1024 * 1024
+LOSS_VMEM = 24 * 1024 * 1024
 
 
 def dot(a, b):
@@ -196,7 +197,7 @@
     slots = positives.shape[0]
     hidden = w_out.shape[0]
     tile = 256
-    any_spec = pl.BlockSpec(memory_space=pl.ANY)
+    any_spec = pl.BlockSpec(memory_space=pltpu.HBM)
     vmem = pl.BlockSpec(memory_space=pltpu.VMEM)
     smem = pl.BlockSpec(memory_space=pltpu.SMEM)
     return pl.pallas_call(
@@ -215,7 +216,7 @@
             pltpu.VMEM((16, width), F32),
             pltpu.SemaphoreType.DMA((8,)),
         ],
-        compiler_params=pltpu.CompilerParams(vmem_limit_bytes=VMEM_LIMIT),
+        compiler_params=pltpu.CompilerParams(vmem_limit_bytes=POOL_VMEM),
         cost_estimate=pl.CostEstimate(
             flops=2 * rows * width * 4 * hidden + 4 * rows * rows * hidden,
             bytes_accessed=2 * (rows * width + 4 * width * hidden),
@@ -341,7 +342,7 @@
             pltpu.VMEM((total, total), F32),
             pltpu.VMEM((total, 128), F32),
         ],
-        compiler_params=pltpu.CompilerParams(vmem_limit_bytes=VMEM_LIMIT),
+        compiler_params=pltpu.CompilerParams(vmem_limit_bytes=LOSS_VMEM),
         cost_estimate=pl.CostEstimate(
             flops=4 * total * total * width,
             bytes_accessed=4 * total * width,
@@ -358,15 +359,17 @@
     plane_size = lax.axis_size(plane)
     packed = pooled_rows(tokens, seg_ids, counts, positives, w_qkv, w_out, ln_gain, z_size)
     padded = packed.shape[-1]
+    w_proj, packed = lax.optimization_barrier((w_proj, packed))
+    gram = lax.dot_general(
+        w_proj, w_proj, (((1,), (1,)), ((), ())), preferred_element_type=F32
+    ).astype(BF16)
     line = lax.all_to_all(packed, "dp_0", split_axis=0, concat_axis=0, tiled=True)
     line = line.reshape(z_size * slots, padded)
     copies = jnp.broadcast_to(line, (plane_size, *line.shape))
     mine = lax.all_to_all(copies, plane, split_axis=0, concat_axis=0, tiled=True)
     mine = mine.reshape(plane_size * z_size * slots, padded)
+    mine, gram = lax.optimization_barrier((mine, gram))
     other = lax.ppermute(mine, "dp_3", [(0, 1), (1, 0)])
-    gram = lax.dot_general(
-        w_proj, w_proj, (((1,), (1,)), ((), ())), preferred_element_type=F32
-    ).astype(BF16)
     return loss_and_grad(mine, other, gram, slots)
 
 

time: 88.7 us -> 80.3 us (0.905)
  blocking collectives: 41.9 us -> 17.5 us
  waiting for transfers between devices: 0.01 us -> 10.9 us
  starting transfers between devices: 2.73 us -> 10.9 us
  Pallas kernels: 33.1 us -> 30.8 us
  matrix products: 9.33 us -> 7.99 us
    all_to_all x1 -> x0, blocking collectives: 25.3 us -> none  [body(): lax.all_to_all(copies, plane, split_axis=0, concat_axis=0, tiled=True)]
    all_to_all x0 -> x1, waiting for transfers between devices: none -> 8.38 us  [body(): lax.all_to_all(copies, plane, split_axis=0, concat_axis=0, tiled=True)]
    all_to_all x0 -> x1, starting transfers between devices: none -> 7.4 us  [body(): lax.all_to_all(copies, plane, split_axis=0, concat_axis=0, tiled=True)]
    ppermute x1, waiting for transfers between devices: 0.01 us -> 2.47 us  [body(): other = lax.ppermute(mine, 'dp_3', [(0, 1), (1, 0)])]
    pallas_call x1, Pallas kernels: 8.61 us -> 6.32 us  [loss_and_grad(): pl.pallas_call(loss_kernel, out_shape=(jax.ShapeDtypeStruct((slots,), F32...]
    dot_general x1, matrix products: 9.33 us -> 7.99 us  [body(): lax.dot_general(w_proj, w_proj, (((1,), (1,)), ((), ())), preferred_eleme...]
    unnamed x4 -> x0, local copies, waits for them, and re-layouts: 1.05 us -> none
    broadcast_in_dim x1, local copies, waits for them, and re-layouts: 0.09 us -> 1.11 us  [body(): copies = jnp.broadcast_to(line, (plane_size, *line.shape))]
  transfers between devices with their start and end apart: 1 -> 2, of which waited for: 0 -> 2; matrix products, arithmetic and copies ran while one was open for 10% -> 10% of each run, Pallas kernels for 0% -> 0%
where the time goes in v2:
time: 80.3 us; the launch traced here: 80 us
  Pallas kernels  30.8 us (38%)
  blocking collectives  17.5 us (22%)
  starting transfers between devices  10.9 us (14%)
  waiting for transfers between devices  10.9 us (14%)
  matrix products  7.99 us (10%)
  local copies, waits for them, and re-layouts  1.13 us (1%)
  between operations  0.84 us (1%)
    pallas_call x1, Pallas kernels, pooled_rows(): pl.pallas_call(functools.partial(pool_kernel, copies=copies, tile=tile),...  24.5 us
    all_to_all x1, blocking collectives, body(): lax.all_to_all(packed, 'dp_0', split_axis=0, concat_axis=0, tiled=True)  17.5 us
    all_to_all x1, waiting for transfers between devices, body(): lax.all_to_all(copies, plane, split_axis=0, concat_axis=0, tiled=True)  8.38 us
    dot_general x1, matrix products, body(): lax.dot_general(w_proj, w_proj, (((1,), (1,)), ((), ())), preferred_eleme...  7.99 us
    all_to_all x1, starting transfers between devices, body(): lax.all_to_all(copies, plane, split_axis=0, concat_axis=0, tiled=True)  7.4 us
    pallas_call x1, Pallas kernels, loss_and_grad(): pl.pallas_call(loss_kernel, out_shape=(jax.ShapeDtypeStruct((slots,), F32...  6.32 us
    ppermute x1, starting transfers between devices, body(): other = lax.ppermute(mine, 'dp_3', [(0, 1), (1, 0)])  3.53 us
    ppermute x1, waiting for transfers between devices, body(): other = lax.ppermute(mine, 'dp_3', [(0, 1), (1, 0)])  2.47 us
  transfers between devices with their start and end apart: 2, of which 2 were waited for; matrix products, arithmetic and copies ran while one was open for 10% of the time, Pallas kernels for 0%

profile of v2, /device:TPU:1, one launch (start us, length us, event | category | flops | bytes accessed | tf_op | source)
XLA Modules:
  0.0 80.0 jit_solution(10833474488559632331)
XLA Ops:
  0.6 24.5 %pool.1 = bf16[8,4,1152]{2,1,0:T(4,128)(2,1)} custom-call(s32[1,1024]{1,0:T(1,128)} %seg_ref.1, s32[256]{0:T(256)} %counts_ref.1, s32[4]{0:T(128)} %positives_ref.1, bf16[1024,1024]{1,0:T(8,128)(2,1)} %x_hbm.1, bf16[1024,1536]{1,0:T(8,128)(2,1)} %wqkv_hbm.1, bf16[512,1024]{1,0:T(8,128)(2,1)} %wout_hbm.1, f32[1,1024]{1,0:T(1,128)} %bitcast.6), custom_call_target="tpu_custom_call" | custom-call | flops 6442450944 | bytes 6291456 | tf_op jit(solution)/shard_map/pool/pallas_call | solution.py:203
  25.1 17.5 %all_to_all.10 = bf16[8,4,1152]{2,1,0:T(4,128)(2,1)S(1)} all-to-all(bf16[8,4,1152]{2,1,0:T(4,128)(2,1)} %pool.1), channel_id=1, replica_groups=mesh['dp_0'=8,'dp_1'=4,'dp_2'=4,'dp_3'=2] {'dp_0'}, dimensions={0} | all-to-all | bytes 147456 | tf_op jit(solution)/shard_map/all_to_all | solution.py:366
  42.7 1.1 %broadcast_in_dim.3 = bf16[16,32,1152]{2,1,0:T(8,128)(2,1)} broadcast(bf16[32,1152]{1,0:T(8,128)(2,1)S(1)} %reshape.14), dimensions={1,2} | broadcast | bytes 1253376 | tf_op jit(solution)/shard_map/broadcast_in_dim | solution.py:368
  43.8 7.4 %all-to-all-start.1 = ((bf16[16,32,1152]{2,1,0:T(8,128)(2,1)}), bf16[16,32,1152]{2,1,0:T(8,128)(2,1)S(1)}, u32[]{:S(2)}, u32[]{:S(2)}) async-start(bf16[16,32,1152]{2,1,0:T(8,128)(2,1)} %broadcast_in_dim.3), calls=%async_computation.1 | async-start | bytes 2359296 | tf_op jit(solution)/shard_map/all_to_all | solution.py:369
  51.2 8.0 %convolution_convert_fusion.gram_ref = bf16[1024,1024]{1,0:T(8,128)(2,1)S(1)} fusion(bf16[1024,2048]{1,0:T(8,128)(2,1)} %param.15), kind=kOutput, calls=%fused_computation | convolution fusion | flops 4296015872 | bytes 6291456 | tf_op jit(solution)/shard_map/dot_general | solution.py:363
  59.2 8.4 %all-to-all-done.1 = bf16[16,32,1152]{2,1,0:T(8,128)(2,1)S(1)} async-done(((bf16[16,32,1152]{2,1,0:T(8,128)(2,1)}), bf16[16,32,1152]{2,1,0:T(8,128)(2,1)S(1)}, u32[]{:S(2)}, u32[]{:S(2)}) %all-to-all-start.1) | async-done | bytes 1179680 | tf_op jit(solution)/shard_map/all_to_all | solution.py:369
  67.5 3.5 %collective-permute-start = (bf16[512,1152]{1,0:T(8,128)(2,1)S(1)}, bf16[512,1152]{1,0:T(8,128)(2,1)S(1)}, u32[]{:S(2)}, u32[]{:S(2)}) collective-permute-start(bf16[512,1152]{1,0:T(8,128)(2,1)S(1)} %bitcast.4), channel_id=1, source_target_pairs={{0,1},{1,0},{2,3},{3,2},{4,5},{5,4},{6,7},{7,6},{8,9},{9,8},{10,11... | collective-permute-start | bytes 3538952 | tf_op jit(solution)/shard_map/ppermute | solution.py:372
  71.1 2.5 %collective-permute-done.other_ref = bf16[512,1152]{1,0:T(8,128)(2,1)S(1)} collective-permute-done((bf16[512,1152]{1,0:T(8,128)(2,1)S(1)}, bf16[512,1152]{1,0:T(8,128)(2,1)S(1)}, u32[]{:S(2)}, u32[]{:S(2)}) %collective-permute-start) | collective-permute-done | bytes 1179680 | tf_op jit(solution)/shard_map/ppermute | solution.py:372
  73.5 6.3 %loss.1 = (f32[4]{0:T(128)}, f32[4,1024]{1,0:T(4,128)}) custom-call(bf16[512,1152]{1,0:T(8,128)(2,1)S(1)} %bitcast.5, bf16[512,1152]{1,0:T(8,128)(2,1)S(1)} %collective-permute-done.other_ref, bf16[1024,1024]{1,0:T(8,128)(2,1)S(1)} %convolution_convert_fusion.gram_ref), custom_call_target="tpu_custom_call" | custom-call | flops 4294967296 | bytes 4194304 | tf_op jit(solution)/shard_map/loss/pallas_call | solution.py:331
  (1 shorter events, 0.0 us)
Async XLA Ops:
  43.8 23.8 %all-to-all-start.1 = ((bf16[16,32,1152]{2,1,0:T(8,128)(2,1)}), bf16[16,32,1152]{2,1,0:T(8,128)(2,1)S(1)}, u32[]{:S(2)}, u32[]{:S(2)}) async-start(bf16[16,32,1152]{2,1,0:T(8,128)(2,1)} %broadcast_in_dim.3), calls=%async_computation.1 | async-start | bytes 2359296 | tf_op jit(solution)/shard_map/all_to_all | solution.py:369
  67.5 6.0 %collective-permute-start = (bf16[512,1152]{1,0:T(8,128)(2,1)S(1)}, bf16[512,1152]{1,0:T(8,128)(2,1)S(1)}, u32[]{:S(2)}, u32[]{:S(2)}) collective-permute-start(bf16[512,1152]{1,0:T(8,128)(2,1)S(1)} %bitcast.4), channel_id=1, source_target_pairs={{0,1},{1,0},{2,3},{3,2},{4,5},{5,4},{6,7},{7,6},{8,9},{9,8},{10,11... | collective-permute-start | bytes 3538952 | tf_op jit(solution)/shard_map/ppermute | solution.py:372

commit v3 on v2

--- a/solution.py
+++ b/solution.py
@@ -16,6 +16,7 @@
 LOG2E = math.log2(math.e)
 LOGIT_SCALE = 20.0
 META = 128
+ONES = 16
 FAR = -1e30
 BF16 = jnp.bfloat16
 F32 = jnp.float32
@@ -29,6 +30,10 @@
 
 def dot_nt(a, b):
     return lax.dot_general(a, b, (((1,), (1,)), ((), ())), preferred_element_type=F32)
+
+
+def dot_tn(a, b):
+    return lax.dot_general(a, b, (((0,), (0,)), ((), ())), preferred_element_type=F32)
 
 
 def rank_of():
@@ -94,16 +99,15 @@
     first_half = lane < HEAD_DIM
 
     x_copy.wait()
-    for c in range(chunks):
-        w_copies[c].wait()
-        kind, place = divmod(c * chunk, hidden)
-        part = dot(x_ref[...], wqkv_ref[:, c * chunk : (c + 1) * chunk])
+    def project(kind, g, carry):
+        c0 = pl.multiple_of(kind * hidden + g * chunk, chunk)
+        part = dot(x_ref[...], wqkv_ref[:, pl.ds(c0, chunk)])
         if kind == 0:
             part = part * (LOG2E * HEAD_DIM**-0.5)
         part = part.astype(BF16)
         for p in range(chunk // (2 * HEAD_DIM)):
             pair = part[:, p * 2 * HEAD_DIM : (p + 1) * 2 * HEAD_DIM]
-            head = place // HEAD_DIM + 2 * p
+            head = g * (chunk // HEAD_DIM) + 2 * p
             if kind == 0:
                 q_ref[head] = jnp.where(first_half, pair, q_mark)
                 q_ref[head + 1] = jnp.where(first_half, q_mark, pair)
@@ -111,19 +115,42 @@
                 k_ref[head] = jnp.where(first_half, pair, k_mark)
                 k_ref[head + 1] = jnp.where(first_half, k_mark, pair)
             else:
-                one = jnp.ones_like(pair)
-                v_ref[head] = jnp.where(first_half, pair, one)
-                v_ref[head + 1] = jnp.where(first_half, one, pair)
+                turned = pair.T
+                for i in range(2):
+                    v_ref[head + i, 0:HEAD_DIM, :] = turned[i * HEAD_DIM : (i + 1) * HEAD_DIM]
+                    v_ref[head + i, HEAD_DIM:, :] = jnp.ones((ONES, rows), BF16)
+        return carry
+
+    for kind in range(3):
+        for c in range(kind * chunks // 3, (kind + 1) * chunks // 3):
+            w_copies[c].wait()
+        lax.fori_loop(0, chunks // 3, functools.partial(project, kind), 0)
 
     wout_copy.wait()
     sums_ref[...] = jnp.zeros_like(sums_ref)
-    half = lax.broadcasted_iota(jnp.int32, (tile, 2 * HEAD_DIM), 1) < HEAD_DIM
+    ctx_ref[...] = jnp.zeros_like(ctx_ref)
     key_tile = 128
     key_tiles = rows // key_tile
     widths = [w for w in (3, 4, 5, 6, 8) if w <= key_tiles]
 
+    def project_out(r0):
+        return x_ref[pl.ds(r0, tile), :].astype(F32) + dot_tn(ctx_ref[...], wout_ref[...])
+
+    def pool_tile(resid, r0, valid):
+        centre = resid - jnp.mean(resid, axis=1, keepdims=True)
+        variance = jnp.mean(centre * centre, axis=1, keepdims=True)
+        out = (centre * lax.rsqrt(variance + 1e-05) * gain_ref[...]).astype(BF16)
+        slot = lax.broadcasted_iota(jnp.int32, (16, tile), 0)
+        token = lax.broadcasted_iota(jnp.int32, (16, tile), 1) + r0
+        member = jnp.zeros((16, tile), jnp.bool_)
+        for s in range(slots):
+            member |= (slot == s) & (token >= begins[s]) & (token < begins[s + 1])
+        member = jnp.where(member & valid, 1.0, 0.0).astype(BF16)
+        sums_ref[...] += dot(member, out)
+
     def one_tile(t, carry):
         r0 = pl.multiple_of(t * tile, tile)
+        last = pl.multiple_of(jnp.maximum(r0 - tile, 0), tile)
         low = jnp.int32(0)
         high = jnp.int32(rows)
         for s in range(1, slots):
@@ -139,33 +166,37 @@
             @pl.when((need > above) & (need <= w))
             def _():
                 start = pl.multiple_of(jnp.minimum(k0, key_tiles - w) * key_tile, key_tile)
-                for p in range(PAIRS):
-                    outs = []
-                    for h in (2 * p, 2 * p + 1):
-                        q = q_ref[h, pl.ds(r0, tile), :]
-                        k = k_ref[h, pl.ds(start, w * key_tile), :]
-                        v = v_ref[h, pl.ds(start, w * key_tile), :]
-                        s = dot_nt(q, k)
-                        e = jnp.exp2(s - jnp.max(s, axis=1, keepdims=True)).astype(BF16)
-                        outs.append(dot(e, v))
-                    top = jnp.where(half, outs[0], outs[1])
-                    bottom = jnp.where(half, outs[1], outs[0])
-                    bottom = pltpu.roll(bottom, HEAD_DIM, 1)
-                    ctx_ref[:, p * 2 * HEAD_DIM : (p + 1) * 2 * HEAD_DIM] = (top / bottom).astype(BF16)
-
-        resid = x_ref[pl.ds(r0, tile), :].astype(F32) + dot(ctx_ref[...], wout_ref[...])
-        centre = resid - jnp.mean(resid, axis=1, keepdims=True)
-        variance = jnp.mean(centre * centre, axis=1, keepdims=True)
-        out = (centre * lax.rsqrt(variance + 1e-05) * gain_ref[...]).astype(BF16)
-        slot = lax.broadcasted_iota(jnp.int32, (16, tile), 0)
-        token = lax.broadcasted_iota(jnp.int32, (16, tile), 1) + r0
-        member = jnp.zeros((16, tile), jnp.bool_)
-        for s in range(slots):
-            member |= (slot == s) & (token >= begins[s]) & (token < begins[s + 1])
-        sums_ref[...] += dot(jnp.where(member, 1.0, 0.0).astype(BF16), out)
+                def score(h):
+                    q = q_ref[h, pl.ds(r0, tile), :]
+                    k = k_ref[h, pl.ds(start, w * key_tile), :]
+                    return dot_nt(k, q)
+
+                def soften(s):
+                    return jnp.exp2(s - jnp.max(s, axis=0, keepdims=True)).astype(BF16)
+
+                def finish(h, e):
+                    v = v_ref[h, :, pl.ds(start, w * key_tile)]
+                    out = dot(v, e)
+                    part = out[0:HEAD_DIM] / out[HEAD_DIM : HEAD_DIM + 1]
+                    ctx_ref[h * HEAD_DIM : (h + 1) * HEAD_DIM, :] = part.astype(BF16)
+
+                resid = project_out(last)
+                ahead = [score(0), score(1)]
+                for h in range(0, HEADS, 2):
+                    now = ahead
+                    if h + 2 < HEADS:
+                        ahead = [score(h + 2), score(h + 3)]
+                    es = [soften(s) for s in now]
+                    for i in range(2):
+                        finish(h + i, es[i])
+                    if h == 2:
+                        pool_tile(resid, last, t > 0)
+
         return carry
 
     lax.fori_loop(0, rows // tile, one_tile, 0)
+    last = rows - tile
+    pool_tile(project_out(last), last, True)
 
     slot_col = lax.broadcasted_iota(jnp.int32, (slots, 1), 0)
     sizes = jnp.ones((slots, 1), F32)
@@ -211,8 +242,8 @@
             pltpu.VMEM((hidden, width), BF16),
             pltpu.VMEM((HEADS, rows, 2 * HEAD_DIM), BF16),
             pltpu.VMEM((HEADS, rows, 2 * HEAD_DIM), BF16),
-            pltpu.VMEM((HEADS, rows, 2 * HEAD_DIM), BF16),
-            pltpu.VMEM((tile, hidden), BF16),
+            pltpu.VMEM((HEADS, HEAD_DIM + ONES, rows), BF16),
+            pltpu.VMEM((hidden, tile), BF16),
             pltpu.VMEM((16, width), F32),
             pltpu.SemaphoreType.DMA((8,)),
         ],

time: 80.3 us -> 72.1 us (0.90)
  Pallas kernels: 30.8 us -> 22.1 us
    pallas_call x1, Pallas kernels: 24.5 us -> 15.8 us  [pooled_rows(): pl.pallas_call(functools.partial(pool_kernel, copies=copies, tile=tile),...]
    all_to_all x1, starting transfers between devices: 7.4 us -> 8.21 us  [body(): lax.all_to_all(copies, plane, split_axis=0, concat_axis=0, tiled=True)]
  transfers between devices with their start and end apart: 2 -> 2, of which waited for: 2 -> 2; matrix products, arithmetic and copies ran while one was open for 10% -> 11% of each run, Pallas kernels for 0% -> 0%
where the time goes in v3:
time: 72.1 us; the launch traced here: 72.4 us
  Pallas kernels  22.1 us (31%)
  blocking collectives  17.5 us (24%)
  waiting for transfers between devices  11.5 us (16%)
  starting transfers between devices  11.4 us (16%)
  matrix products  7.99 us (11%)
  local copies, waits for them, and re-layouts  1.13 us (2%)
  between operations  0.82 us (1%)
    all_to_all x1, blocking collectives, body(): lax.all_to_all(packed, 'dp_0', split_axis=0, concat_axis=0, tiled=True)  17.5 us
    pallas_call x1, Pallas kernels, pooled_rows(): pl.pallas_call(functools.partial(pool_kernel, copies=copies, tile=tile),...  15.8 us
    all_to_all x1, waiting for transfers between devices, body(): lax.all_to_all(copies, plane, split_axis=0, concat_axis=0, tiled=True)  8.99 us
    all_to_all x1, starting transfers between devices, body(): lax.all_to_all(copies, plane, split_axis=0, concat_axis=0, tiled=True)  8.21 us
    dot_general x1, matrix products, body(): lax.dot_general(w_proj, w_proj, (((1,), (1,)), ((), ())), preferred_eleme...  7.99 us
    pallas_call x1, Pallas kernels, loss_and_grad(): pl.pallas_call(loss_kernel, out_shape=(jax.ShapeDtypeStruct((slots,), F32...  6.32 us
    ppermute x1, starting transfers between devices, body(): other = lax.ppermute(mine, 'dp_3', [(0, 1), (1, 0)])  3.17 us
    ppermute x1, waiting for transfers between devices, body(): other = lax.ppermute(mine, 'dp_3', [(0, 1), (1, 0)])  2.47 us
  transfers between devices with their start and end apart: 2, of which 2 were waited for; matrix products, arithmetic and copies ran while one was open for 11% of the time, Pallas kernels for 0%

profile of v3, /device:TPU:1, one launch (start us, length us, event | category | flops | bytes accessed | tf_op | source)
XLA Modules:
  0.0 72.4 jit_solution(4991814056933899127)
XLA Ops:
  0.6 15.8 %pool.1 = bf16[8,4,1152]{2,1,0:T(4,128)(2,1)} custom-call(s32[1,1024]{1,0:T(1,128)} %seg_ref.1, s32[256]{0:T(256)} %counts_ref.1, s32[4]{0:T(128)} %positives_ref.1, bf16[1024,1024]{1,0:T(8,128)(2,1)} %x_hbm.1, bf16[1024,1536]{1,0:T(8,128)(2,1)} %wqkv_hbm.1, bf16[512,1024]{1,0:T(8,128)(2,1)} %wout_hbm.1, f32[1,1024]{1,0:T(1,128)} %bitcast.6), custom_call_target="tpu_custom_call" | custom-call | flops 6442450944 | bytes 6291456 | tf_op jit(solution)/shard_map/pool/pallas_call | solution.py:234
  16.4 17.5 %all_to_all.10 = bf16[8,4,1152]{2,1,0:T(4,128)(2,1)S(1)} all-to-all(bf16[8,4,1152]{2,1,0:T(4,128)(2,1)} %pool.1), channel_id=1, replica_groups=mesh['dp_0'=8,'dp_1'=4,'dp_2'=4,'dp_3'=2] {'dp_0'}, dimensions={0} | all-to-all | bytes 147456 | tf_op jit(solution)/shard_map/all_to_all | solution.py:397
  34.0 1.1 %broadcast_in_dim.3 = bf16[16,32,1152]{2,1,0:T(8,128)(2,1)} broadcast(bf16[32,1152]{1,0:T(8,128)(2,1)S(1)} %reshape.14), dimensions={1,2} | broadcast | bytes 1253376 | tf_op jit(solution)/shard_map/broadcast_in_dim | solution.py:399
  35.1 8.2 %all-to-all-start.1 = ((bf16[16,32,1152]{2,1,0:T(8,128)(2,1)}), bf16[16,32,1152]{2,1,0:T(8,128)(2,1)S(1)}, u32[]{:S(2)}, u32[]{:S(2)}) async-start(bf16[16,32,1152]{2,1,0:T(8,128)(2,1)} %broadcast_in_dim.3), calls=%async_computation.1 | async-start | bytes 2359296 | tf_op jit(solution)/shard_map/all_to_all | solution.py:400
  43.3 8.0 %convolution_convert_fusion.gram_ref = bf16[1024,1024]{1,0:T(8,128)(2,1)S(1)} fusion(bf16[1024,2048]{1,0:T(8,128)(2,1)} %param.15), kind=kOutput, calls=%fused_computation | convolution fusion | flops 4296015872 | bytes 6291456 | tf_op jit(solution)/shard_map/dot_general | solution.py:394
  51.3 9.0 %all-to-all-done.1 = bf16[16,32,1152]{2,1,0:T(8,128)(2,1)S(1)} async-done(((bf16[16,32,1152]{2,1,0:T(8,128)(2,1)}), bf16[16,32,1152]{2,1,0:T(8,128)(2,1)S(1)}, u32[]{:S(2)}, u32[]{:S(2)}) %all-to-all-start.1) | async-done | bytes 1179680 | tf_op jit(solution)/shard_map/all_to_all | solution.py:400
  60.3 3.2 %collective-permute-start = (bf16[512,1152]{1,0:T(8,128)(2,1)S(1)}, bf16[512,1152]{1,0:T(8,128)(2,1)S(1)}, u32[]{:S(2)}, u32[]{:S(2)}) collective-permute-start(bf16[512,1152]{1,0:T(8,128)(2,1)S(1)} %bitcast.4), channel_id=1, source_target_pairs={{0,1},{1,0},{2,3},{3,2},{4,5},{5,4},{6,7},{7,6},{8,9},{9,8},{10,11... | collective-permute-start | bytes 3538952 | tf_op jit(solution)/shard_map/ppermute | solution.py:403
  63.5 2.5 %collective-permute-done.other_ref = bf16[512,1152]{1,0:T(8,128)(2,1)S(1)} collective-permute-done((bf16[512,1152]{1,0:T(8,128)(2,1)S(1)}, bf16[512,1152]{1,0:T(8,128)(2,1)S(1)}, u32[]{:S(2)}, u32[]{:S(2)}) %collective-permute-start) | collective-permute-done | bytes 1179680 | tf_op jit(solution)/shard_map/ppermute | solution.py:403
  65.9 6.3 %loss.1 = (f32[4]{0:T(128)}, f32[4,1024]{1,0:T(4,128)}) custom-call(bf16[512,1152]{1,0:T(8,128)(2,1)S(1)} %bitcast.5, bf16[512,1152]{1,0:T(8,128)(2,1)S(1)} %collective-permute-done.other_ref, bf16[1024,1024]{1,0:T(8,128)(2,1)S(1)} %convolution_convert_fusion.gram_ref), custom_call_target="tpu_custom_call" | custom-call | flops 4294967296 | bytes 4194304 | tf_op jit(solution)/shard_map/loss/pallas_call | solution.py:362
  (1 shorter events, 0.0 us)
Async XLA Ops:
  35.1 25.2 %all-to-all-start.1 = ((bf16[16,32,1152]{2,1,0:T(8,128)(2,1)}), bf16[16,32,1152]{2,1,0:T(8,128)(2,1)S(1)}, u32[]{:S(2)}, u32[]{:S(2)}) async-start(bf16[16,32,1152]{2,1,0:T(8,128)(2,1)} %broadcast_in_dim.3), calls=%async_computation.1 | async-start | bytes 2359296 | tf_op jit(solution)/shard_map/all_to_all | solution.py:400
  60.3 5.6 %collective-permute-start = (bf16[512,1152]{1,0:T(8,128)(2,1)S(1)}, bf16[512,1152]{1,0:T(8,128)(2,1)S(1)}, u32[]{:S(2)}, u32[]{:S(2)}) collective-permute-start(bf16[512,1152]{1,0:T(8,128)(2,1)S(1)} %bitcast.4), channel_id=1, source_target_pairs={{0,1},{1,0},{2,3},{3,2},{4,5},{5,4},{6,7},{7,6},{8,9},{9,8},{10,11... | collective-permute-start | bytes 3538952 | tf_op jit(solution)/shard_map/ppermute | solution.py:403

commit v4 on v3

--- a/solution.py
+++ b/solution.py
@@ -22,6 +22,8 @@
 F32 = jnp.float32
 POOL_VMEM = 60 * 1024 * 1024
 LOSS_VMEM = 24 * 1024 * 1024
+GRAM_VMEM = 12 * 1024 * 1024
+SIDE_VMEM = 12 * 1024 * 1024
 
 
 def dot(a, b):
@@ -257,10 +259,81 @@
     )(seg_ids, counts, positives, tokens, w_qkv, w_out, ln_gain.reshape(1, width))
 
 
+def gram_kernel(w_ref, out_ref, *, block):
+    for b in range(out_ref.shape[0] // block):
+        right = w_ref[b * block : (b + 1) * block, :]
+        for c in range(b + 1):
+            left = w_ref[c * block : (c + 1) * block, :]
+            value = dot_nt(left, right).astype(BF16)
+            out_ref[c * block : (c + 1) * block, b * block : (b + 1) * block] = value
+            if c < b:
+                out_ref[b * block : (b + 1) * block, c * block : (c + 1) * block] = value.T
+
+
+def gram_of(w_proj):
+    rows, depth = w_proj.shape
+    vmem = pl.BlockSpec(memory_space=pltpu.VMEM)
+    return pl.pallas_call(
+        functools.partial(gram_kernel, block=256),
+        out_shape=jax.ShapeDtypeStruct((rows, rows), BF16),
+        in_specs=[vmem],
+        out_specs=vmem,
+        compiler_params=pltpu.CompilerParams(vmem_limit_bytes=GRAM_VMEM),
+        cost_estimate=pl.CostEstimate(
+            flops=2 * rows * rows * depth, bytes_accessed=2 * rows * depth, transcendentals=0
+        ),
+        name="gram",
+    )(w_proj)
+
+
+def side_kernel(pooled_ref, gram_ref, left_ref, right_ref, norm_ref, *, block):
+    sides(pooled_ref, gram_ref[...], left_ref, right_ref, norm_ref, 0, block)
+
+
+def sides(pooled_ref, gram, left_ref, right_ref, norm_ref, place, block):
+    width = gram.shape[0]
+    for begin in range(0, pooled_ref.shape[0], block):
+        rows = slice(place + begin, place + begin + block)
+        pooled = pooled_ref[begin : begin + block, 0:width]
+        through = dot(pooled, gram)
+        wide = pooled.astype(F32)
+        square = jnp.sum(through * wide, axis=1, keepdims=True)
+        rnorm = lax.rsqrt(jnp.maximum(square, 0.0) + 1e-06)
+        left_ref[rows, :] = (through * (rnorm * (LOGIT_SCALE * LOG2E))).astype(BF16)
+        right_ref[rows, :] = (wide * rnorm).astype(BF16)
+        norm_ref[rows, :] = jnp.broadcast_to(rnorm, (block, norm_ref.shape[1]))
+
+
+def own_sides(mine, gram):
+    part = mine.shape[0]
+    width = gram.shape[0]
+    vmem = pl.BlockSpec(memory_space=pltpu.VMEM)
+    return pl.pallas_call(
+        functools.partial(side_kernel, block=256),
+        out_shape=(
+            jax.ShapeDtypeStruct((part, width), BF16),
+            jax.ShapeDtypeStruct((part, width), BF16),
+            jax.ShapeDtypeStruct((part, 128), F32),
+        ),
+        in_specs=[vmem, vmem],
+        out_specs=(vmem, vmem, vmem),
+        compiler_params=pltpu.CompilerParams(vmem_limit_bytes=SIDE_VMEM),
+        cost_estimate=pl.CostEstimate(
+            flops=2 * part * width * width,
+            bytes_accessed=8 * part * width,
+            transcendentals=part,
+        ),
+        name="sides",
+    )(mine, gram)
+
+
 def loss_kernel(
     mine_ref,
     other_ref,
     gram_ref,
+    own_left_ref,
+    own_right_ref,
+    own_norm_ref,
     loss_ref,
     grad_ref,
     left_ref,
@@ -268,24 +341,14 @@
     logit_ref,
     norm_ref,
 ):
-    total, width = left_ref.shape
+    total, width = right_ref.shape
     part = total // 2
     slots = grad_ref.shape[0]
     block = 256
     gram = gram_ref[...]
 
-    for b in range(total // block):
-        ref = mine_ref if b * block < part else other_ref
-        begin = b * block % part
-        rows = slice(b * block, (b + 1) * block)
-        pooled = ref[begin : begin + block, 0:width]
-        through = dot(pooled, gram)
-        wide = pooled.astype(F32)
-        square = jnp.sum(through * wide, axis=1, keepdims=True)
-        rnorm = lax.rsqrt(jnp.maximum(square, 0.0) + 1e-06)
-        left_ref[rows, :] = (through * (rnorm * (LOGIT_SCALE * LOG2E))).astype(BF16)
-        right_ref[rows, :] = (wide * rnorm).astype(BF16)
-        norm_ref[rows, :] = jnp.broadcast_to(rnorm, (block, 128))
+    right_ref[0:part, :] = own_right_ref[...]
+    sides(other_ref, gram, left_ref, right_ref, norm_ref, part, block)
 
     meta = jnp.concatenate([mine_ref[:, width:], other_ref[:, width:]], axis=0)
     pick = lax.broadcasted_iota(jnp.int32, (16, META), 0) == lax.broadcasted_iota(
@@ -299,7 +362,8 @@
     sums = jnp.zeros((8, total), F32)
     for b in range(total // block):
         rows = slice(b * block, (b + 1) * block)
-        logit = dot_nt(left_ref[rows, :], right)
+        left = own_left_ref[rows, :] if b * block < part else left_ref[rows, :]
+        logit = dot_nt(left, right)
         logit_ref[rows, :] = logit
         live = live_col[rows, :]
         pieces = []
@@ -344,9 +408,9 @@
     weights = (query_weights + key_weights).astype(BF16)
     mix = dot(weights, right)
     image = dot(mix.astype(BF16), gram) * LOGIT_SCALE
-    unit_image = left_ref[pl.ds(base, 16), :].astype(F32) * (1.0 / (LOGIT_SCALE * LOG2E))
+    unit_image = own_left_ref[pl.ds(base, 16), :].astype(F32) * (1.0 / (LOGIT_SCALE * LOG2E))
     radial = LOGIT_SCALE * jnp.sum(mix * unit_image, axis=1, keepdims=True)
-    rnorm = norm_ref[pl.ds(base, 16), 0:1]
+    rnorm = own_norm_ref[pl.ds(base, 16), 0:1]
     grad = (image - radial * unit_image) * rnorm
     out = grad[0:slots]
     for i in range(1, 16 // slots):
@@ -354,7 +418,7 @@
     grad_ref[...] = out
 
 
-def loss_and_grad(mine, other, gram, slots):
+def loss_and_grad(mine, other, gram, own, slots):
     part, padded = mine.shape
     width = padded - META
     total = 2 * part
@@ -365,7 +429,7 @@
             jax.ShapeDtypeStruct((slots,), F32),
             jax.ShapeDtypeStruct((slots, width), F32),
         ),
-        in_specs=[vmem, vmem, vmem],
+        in_specs=[vmem] * 6,
         out_specs=(pl.BlockSpec(memory_space=pltpu.SMEM), vmem),
         scratch_shapes=[
             pltpu.VMEM((total, width), BF16),
@@ -380,7 +444,7 @@
             transcendentals=total * total,
         ),
         name="loss",
-    )(mine, other, gram)
+    )(mine, other, gram, *own)
 
 
 def body(tokens, seg_ids, counts, positives, w_qkv, w_out, ln_gain, w_proj):
@@ -391,17 +455,16 @@
     packed = pooled_rows(tokens, seg_ids, counts, positives, w_qkv, w_out, ln_gain, z_size)
     padded = packed.shape[-1]
     w_proj, packed = lax.optimization_barrier((w_proj, packed))
-    gram = lax.dot_general(
-        w_proj, w_proj, (((1,), (1,)), ((), ())), preferred_element_type=F32
-    ).astype(BF16)
+    gram = gram_of(w_proj)
     line = lax.all_to_all(packed, "dp_0", split_axis=0, concat_axis=0, tiled=True)
     line = line.reshape(z_size * slots, padded)
+    line, gram = lax.optimization_barrier((line, gram))
     copies = jnp.broadcast_to(line, (plane_size, *line.shape))
     mine = lax.all_to_all(copies, plane, split_axis=0, concat_axis=0, tiled=True)
     mine = mine.reshape(plane_size * z_size * slots, padded)
-    mine, gram = lax.optimization_barrier((mine, gram))
     other = lax.ppermute(mine, "dp_3", [(0, 1), (1, 0)])
-    return loss_and_grad(mine, other, gram, slots)
+    own = own_sides(mine, gram)
+    return loss_and_grad(mine, other, gram, own, slots)
 
 
 def solution(mesh):

time: 72.1 us -> 69.3 us (0.961)
  waiting for transfers between devices: 11.5 us -> 3.09 us
  matrix products: 7.99 us -> 0 us
  blocking collectives: 17.5 us -> 24 us
  Pallas kernels: 22.1 us -> 27.1 us
  local copies, waits for them, and re-layouts: 1.13 us -> 2.29 us
    dot_general x1 -> x0, matrix products: 7.99 us -> none  [body(): lax.dot_general(w_proj, w_proj, (((1,), (1,)), ((), ())), preferred_eleme...]
    all_to_all x1, waiting for transfers between devices: 8.99 us -> 2.15 us  [body(): lax.all_to_all(packed, 'dp_0', split_axis=0, concat_axis=0, tiled=True)]
    all_to_all x1, blocking collectives: 17.5 us -> 24 us  [body(): lax.all_to_all(copies, plane, split_axis=0, concat_axis=0, tiled=True)]
    pallas_call x0 -> x2, Pallas kernels: none -> 4.5 us  [the longest x1 2.97 us: gram_of(): pl.pallas_call(functools.partial(gram_kernel, block=256), out_shape=jax.S...]
    unnamed x0 -> x2, local copies, waits for them, and re-layouts: none -> 2.18 us
    pallas_call x1, Pallas kernels: 15.8 us -> 17.5 us  [pooled_rows(): pl.pallas_call(functools.partial(pool_kernel, copies=copies, tile=tile),...]
    ppermute x1, waiting for transfers between devices: 2.47 us -> 0.93 us  [body(): other = lax.ppermute(mine, 'dp_3', [(0, 1), (1, 0)])]
    pallas_call x1, Pallas kernels: 6.32 us -> 5.17 us  [loss_and_grad(): pl.pallas_call(loss_kernel, out_shape=(jax.ShapeDtypeStruct((slots,), F32...]
  transfers between devices with their start and end apart: 2 -> 2, of which waited for: 2 -> 2; matrix products, arithmetic and copies ran while one was open for 11% -> 0% of each run, Pallas kernels for 0% -> 7%
where the time goes in v4:
time: 69.3 us; the launch traced here: 68.9 us
  Pallas kernels  27.1 us (39%)
  blocking collectives  24 us (35%)
  starting transfers between devices  11.6 us (17%)
  waiting for transfers between devices  3.09 us (4%)
  local copies, waits for them, and re-layouts  2.29 us (3%)
  between operations  0.83 us (1%)
    all_to_all x1, blocking collectives, body(): lax.all_to_all(copies, plane, split_axis=0, concat_axis=0, tiled=True)  24 us
    pallas_call x1, Pallas kernels, pooled_rows(): pl.pallas_call(functools.partial(pool_kernel, copies=copies, tile=tile),...  17.5 us
    all_to_all x1, starting transfers between devices, body(): lax.all_to_all(packed, 'dp_0', split_axis=0, concat_axis=0, tiled=True)  8.58 us
    pallas_call x1, Pallas kernels, loss_and_grad(): pl.pallas_call(loss_kernel, out_shape=(jax.ShapeDtypeStruct((slots,), F32...  5.17 us
    ppermute x1, starting transfers between devices, body(): other = lax.ppermute(mine, 'dp_3', [(0, 1), (1, 0)])  3.04 us
    pallas_call x1, Pallas kernels, gram_of(): pl.pallas_call(functools.partial(gram_kernel, block=256), out_shape=jax.S...  2.97 us
    unnamed x2, local copies, waits for them, and re-layouts  2.18 us
    all_to_all x1, waiting for transfers between devices, body(): lax.all_to_all(packed, 'dp_0', split_axis=0, concat_axis=0, tiled=True)  2.15 us
  transfers between devices with their start and end apart: 2, of which 2 were waited for; matrix products, arithmetic and copies ran while one was open for 0% of the time, Pallas kernels for 7%

profile of v4, /device:TPU:1, one launch (start us, length us, event | category | flops | bytes accessed | tf_op | source)
XLA Modules:
  0.0 68.9 jit_solution(949814348743814332)
XLA Ops:
  0.6 17.5 %pool.1 = bf16[8,4,1152]{2,1,0:T(4,128)(2,1)} custom-call(s32[1,1024]{1,0:T(1,128)} %seg_ref.1, s32[256]{0:T(256)} %counts_ref.1, s32[4]{0:T(128)} %positives_ref.1, bf16[1024,1024]{1,0:T(8,128)(2,1)} %x_hbm.1, bf16[1024,1536]{1,0:T(8,128)(2,1)} %wqkv_hbm.1, bf16[512,1024]{1,0:T(8,128)(2,1)} %wout_hbm.1, f32[1,1024]{1,0:T(1,128)} %bitcast.5), custom_call_target="tpu_custom_call" | custom-call | flops 6442450944 | bytes 6291456 | tf_op jit(solution)/shard_map/pool/pallas_call | solution.py:236
  18.1 8.6 %all-to-all-start = ((bf16[8,4,1152]{2,1,0:T(4,128)(2,1)}), bf16[8,4,1152]{2,1,0:T(4,128)(2,1)S(1)}, u32[]{:S(2)}, u32[]{:S(2)}) async-start(bf16[8,4,1152]{2,1,0:T(4,128)(2,1)} %pool.1), calls=%async_computation | async-start | bytes 147456 | tf_op jit(solution)/shard_map/all_to_all | solution.py:459
  26.7 0.0 copy-start
  26.7 2.2 %copy-done = bf16[1024,2048]{1,0:T(8,128)(2,1)S(1)} copy-done((bf16[1024,2048]{1,0:T(8,128)(2,1)S(1)}, bf16[1024,2048]{1,0:T(8,128)(2,1)}, u32[]{:S(2)}) %copy-start) | copy-done | bytes 4194328
  28.9 3.0 %gram.1.gram_ref = bf16[1024,1024]{1,0:T(8,128)(2,1)S(1)} custom-call(bf16[1024,2048]{1,0:T(8,128)(2,1)S(1)} %copy-done), custom_call_target="tpu_custom_call" | custom-call | flops 4294967296 | bytes 4194304 | tf_op jit(solution)/shard_map/gram/pallas_call | solution.py:276
  31.8 2.2 %all-to-all-done = bf16[8,4,1152]{2,1,0:T(4,128)(2,1)S(1)} async-done(((bf16[8,4,1152]{2,1,0:T(4,128)(2,1)}), bf16[8,4,1152]{2,1,0:T(4,128)(2,1)S(1)}, u32[]{:S(2)}, u32[]{:S(2)}) %all-to-all-start) | async-done | bytes 73760 | tf_op jit(solution)/shard_map/all_to_all | solution.py:459
  34.0 0.1 broadcast_in_dim.3
  34.1 24.0 %all_to_all.10 = bf16[16,32,1152]{2,1,0:T(8,128)(2,1)S(1)} all-to-all(bf16[16,32,1152]{2,1,0:T(8,128)(2,1)S(1)} %broadcast_in_dim.3), channel_id=1, replica_groups=mesh['dp_0'=8,'dp_1'=4,'dp_2'=4,'dp_3'=2] {'dp_1','dp_2'}, dimensions={0} | all-to-all | bytes 2359296 | tf_op jit(solution)/shard_map/all_to_all | solution.py:463
  58.1 3.0 %collective-permute-start = (bf16[512,1152]{1,0:T(8,128)(2,1)S(1)}, bf16[512,1152]{1,0:T(8,128)(2,1)S(1)}, u32[]{:S(2)}, u32[]{:S(2)}) collective-permute-start(bf16[512,1152]{1,0:T(8,128)(2,1)S(1)} %bitcast.2), channel_id=1, source_target_pairs={{0,1},{1,0},{2,3},{3,2},{4,5},{5,4},{6,7},{7,6},{8,9},{9,8},{10,11... | collective-permute-start | bytes 3538952 | tf_op jit(solution)/shard_map/ppermute | solution.py:465
  61.1 1.5 %sides.1 = (bf16[512,1024]{1,0:T(8,128)(2,1)S(1)}, bf16[512,1024]{1,0:T(8,128)(2,1)S(1)}, f32[512,128]{1,0:T(8,128)S(1)}) custom-call(bf16[512,1152]{1,0:T(8,128)(2,1)S(1)} %bitcast.3, bf16[1024,1024]{1,0:T(8,128)(2,1)S(1)} %gram.1.gram_ref), custom_call_target="tpu_custom_call" | custom-call | flops 1073741824 | bytes 4194304 | tf_op jit(solution)/shard_map/sides/pallas_call | solution.py:311
  62.7 0.9 %collective-permute-done.other_ref = bf16[512,1152]{1,0:T(8,128)(2,1)S(1)} collective-permute-done((bf16[512,1152]{1,0:T(8,128)(2,1)S(1)}, bf16[512,1152]{1,0:T(8,128)(2,1)S(1)}, u32[]{:S(2)}, u32[]{:S(2)}) %collective-permute-start) | collective-permute-done | bytes 1179680 | tf_op jit(solution)/shard_map/ppermute | solution.py:465
  63.6 5.2 %loss.1 = (f32[4]{0:T(128)}, f32[4,1024]{1,0:T(4,128)}) custom-call(bf16[512,1152]{1,0:T(8,128)(2,1)S(1)} %bitcast.4, bf16[512,1152]{1,0:T(8,128)(2,1)S(1)} %collective-permute-done.other_ref, bf16[1024,1024]{1,0:T(8,128)(2,1)S(1)} %gram.1.gram_ref, bf16[512,1024]{1,0:T(8,128)(2,1)S(1)} %get-tuple-element.13.own_left_ref, ...), custom_call_target="tpu_custom_call" | custom-call | flops 4294967296 | bytes 4194304 | tf_op jit(solution)/shard_map/loss/pallas_call | solution.py:426
  (1 shorter events, 0.0 us)
Async XLA Ops:
  18.1 15.9 %all-to-all-start = ((bf16[8,4,1152]{2,1,0:T(4,128)(2,1)}), bf16[8,4,1152]{2,1,0:T(4,128)(2,1)S(1)}, u32[]{:S(2)}, u32[]{:S(2)}) async-start(bf16[8,4,1152]{2,1,0:T(4,128)(2,1)} %pool.1), calls=%async_computation | async-start | bytes 147456 | tf_op jit(solution)/shard_map/all_to_all | solution.py:459
  26.7 2.2 %copy-start = (bf16[1024,2048]{1,0:T(8,128)(2,1)S(1)}, bf16[1024,2048]{1,0:T(8,128)(2,1)}, u32[]{:S(2)}) copy-start(bf16[1024,2048]{1,0:T(8,128)(2,1)} %w_ref) | copy-start | bytes 12582916
  58.1 5.5 %collective-permute-start = (bf16[512,1152]{1,0:T(8,128)(2,1)S(1)}, bf16[512,1152]{1,0:T(8,128)(2,1)S(1)}, u32[]{:S(2)}, u32[]{:S(2)}) collective-permute-start(bf16[512,1152]{1,0:T(8,128)(2,1)S(1)} %bitcast.2), channel_id=1, source_target_pairs={{0,1},{1,0},{2,3},{3,2},{4,5},{5,4},{6,7},{7,6},{8,9},{9,8},{10,11... | collective-permute-start | bytes 3538952 | tf_op jit(solution)/shard_map/ppermute | solution.py:465

commit v5 on v4

--- a/solution.py
+++ b/solution.py
@@ -68,20 +68,25 @@
     rows, width = x_ref.shape
     slots = out_ref.shape[1]
     hidden = HEADS * HEAD_DIM
-    chunk = 256
+    chunk = 512
     chunks = 3 * hidden // chunk
 
-    x_copy = pltpu.make_async_copy(x_hbm, x_ref, sems.at[0])
-    x_copy.start()
+    parts = 2
+    x_copies = []
+    for r in range(parts):
+        some = slice(r * rows // parts, (r + 1) * rows // parts)
+        x_copies.append(
+            pltpu.make_async_copy(x_hbm.at[some, :], x_ref.at[some, :], sems.at[r])
+        )
     w_copies = []
     for c in range(chunks):
         cols = slice(c * chunk, (c + 1) * chunk)
         w_copies.append(
-            pltpu.make_async_copy(wqkv_hbm.at[:, cols], wqkv_ref.at[:, cols], sems.at[1 + c])
+            pltpu.make_async_copy(wqkv_hbm.at[:, cols], wqkv_ref.at[:, cols], sems.at[parts + c])
         )
-        w_copies[-1].start()
-    wout_copy = pltpu.make_async_copy(wout_hbm, wout_ref, sems.at[1 + chunks])
-    wout_copy.start()
+    wout_copy = pltpu.make_async_copy(wout_hbm, wout_ref, sems.at[parts + chunks])
+    for copy in [w_copies[0], *x_copies, *w_copies[1:], wout_copy]:
+        copy.start()
 
     seg = seg_ref[...]
     begins = [jnp.int32(0)]
@@ -100,33 +105,37 @@
     k_mark = jnp.where(mine | (feature >= slots), 0.0, FAR).astype(BF16)
     first_half = lane < HEAD_DIM
 
-    x_copy.wait()
-    def project(kind, g, carry):
+    def project(kind, some, g, carry):
         c0 = pl.multiple_of(kind * hidden + g * chunk, chunk)
-        part = dot(x_ref[...], wqkv_ref[:, pl.ds(c0, chunk)])
+        part = dot(x_ref[some, :], wqkv_ref[:, pl.ds(c0, chunk)])
         if kind == 0:
             part = part * (LOG2E * HEAD_DIM**-0.5)
         part = part.astype(BF16)
+        left = first_half[some]
         for p in range(chunk // (2 * HEAD_DIM)):
             pair = part[:, p * 2 * HEAD_DIM : (p + 1) * 2 * HEAD_DIM]
             head = g * (chunk // HEAD_DIM) + 2 * p
             if kind == 0:
-                q_ref[head] = jnp.where(first_half, pair, q_mark)
-                q_ref[head + 1] = jnp.where(first_half, q_mark, pair)
+                q_ref[head, some, :] = jnp.where(left, pair, q_mark[some])
+                q_ref[head + 1, some, :] = jnp.where(left, q_mark[some], pair)
             elif kind == 1:
-                k_ref[head] = jnp.where(first_half, pair, k_mark)
-                k_ref[head + 1] = jnp.where(first_half, k_mark, pair)
+                k_ref[head, some, :] = jnp.where(left, pair, k_mark[some])
+                k_ref[head + 1, some, :] = jnp.where(left, k_mark[some], pair)
             else:
                 turned = pair.T
                 for i in range(2):
-                    v_ref[head + i, 0:HEAD_DIM, :] = turned[i * HEAD_DIM : (i + 1) * HEAD_DIM]
-                    v_ref[head + i, HEAD_DIM:, :] = jnp.ones((ONES, rows), BF16)
+                    v_ref[head + i, 0:HEAD_DIM, some] = turned[i * HEAD_DIM : (i + 1) * HEAD_DIM]
+                    v_ref[head + i, HEAD_DIM:, some] = jnp.ones((ONES, turned.shape[1]), BF16)
         return carry
 
-    for kind in range(3):
-        for c in range(kind * chunks // 3, (kind + 1) * chunks // 3):
-            w_copies[c].wait()
-        lax.fori_loop(0, chunks // 3, functools.partial(project, kind), 0)
+    w_copies[0].wait()
+    for r in range(parts):
+        x_copies[r].wait()
+        project(0, slice(r * rows // parts, (r + 1) * rows // parts), 0, 0)
+    for kind in (1, 2):
+        w_copies[kind].wait()
+        for r in range(parts):
+            project(kind, slice(r * rows // parts, (r + 1) * rows // parts), 0, 0)
 
     wout_copy.wait()
     sums_ref[...] = jnp.zeros_like(sums_ref)
@@ -183,16 +192,18 @@
                     ctx_ref[h * HEAD_DIM : (h + 1) * HEAD_DIM, :] = part.astype(BF16)
 
                 resid = project_out(last)
-                ahead = [score(0), score(1)]
-                for h in range(0, HEADS, 2):
-                    now = ahead
-                    if h + 2 < HEADS:
-                        ahead = [score(h + 2), score(h + 3)]
-                    es = [soften(s) for s in now]
-                    for i in range(2):
-                        finish(h + i, es[i])
+                scores = [score(h) for h in range(4)]
+                soft = []
+                for h in range(HEADS):
+                    if h + 4 < HEADS:
+                        scores.append(score(h + 4))
+                    soft.append(soften(scores[h]))
+                    if h >= 2:
+                        finish(h - 2, soft[h - 2])
                     if h == 2:
                         pool_tile(resid, last, t > 0)
+                for h in range(HEADS - 2, HEADS):
+                    finish(h, soft[h])
 
         return carry
 

time: 69.3 us -> 67.8 us (0.978)
  blocking collectives: 24 us -> 23.2 us
    all_to_all x1, blocking collectives: 24 us -> 23.2 us  [body(): lax.all_to_all(copies, plane, split_axis=0, concat_axis=0, tiled=True)]
where the time goes in v5:
time: 67.8 us; the launch traced here: 67.7 us
  Pallas kernels  26.7 us (39%)
  blocking collectives  23.2 us (34%)
  starting transfers between devices  11.6 us (17%)
  waiting for transfers between devices  3.09 us (5%)
  local copies, waits for them, and re-layouts  2.29 us (3%)
  between operations  0.85 us (1%)
    all_to_all x1, blocking collectives, body(): lax.all_to_all(copies, plane, split_axis=0, concat_axis=0, tiled=True)  23.2 us
    pallas_call x1, Pallas kernels, pooled_rows(): pl.pallas_call(functools.partial(pool_kernel, copies=copies, tile=tile),...  17 us
    all_to_all x1, starting transfers between devices, body(): lax.all_to_all(packed, 'dp_0', split_axis=0, concat_axis=0, tiled=True)  7.99 us
    pallas_call x1, Pallas kernels, loss_and_grad(): pl.pallas_call(loss_kernel, out_shape=(jax.ShapeDtypeStruct((slots,), F32...  5.17 us
    ppermute x1, starting transfers between devices, body(): other = lax.ppermute(mine, 'dp_3', [(0, 1), (1, 0)])  3.57 us
    pallas_call x1, Pallas kernels, gram_of(): pl.pallas_call(functools.partial(gram_kernel, block=256), out_shape=jax.S...  2.96 us
    unnamed x2, local copies, waits for them, and re-layouts  2.18 us
    all_to_all x1, waiting for transfers between devices, body(): lax.all_to_all(packed, 'dp_0', split_axis=0, concat_axis=0, tiled=True)  2.16 us
  transfers between devices with their start and end apart: 2, of which 2 were waited for; matrix products, arithmetic and copies ran while one was open for 0% of the time, Pallas kernels for 7%

profile of v5, /device:TPU:1, one launch (start us, length us, event | category | flops | bytes accessed | tf_op | source)
XLA Modules:
  0.0 67.7 jit_solution(11486872493742344680)
XLA Ops:
  0.6 17.0 %pool.1 = bf16[8,4,1152]{2,1,0:T(4,128)(2,1)} custom-call(s32[1,1024]{1,0:T(1,128)} %seg_ref.1, s32[256]{0:T(256)} %counts_ref.1, s32[4]{0:T(128)} %positives_ref.1, bf16[1024,1024]{1,0:T(8,128)(2,1)} %x_hbm.1, bf16[1024,1536]{1,0:T(8,128)(2,1)} %wqkv_hbm.1, bf16[512,1024]{1,0:T(8,128)(2,1)} %wout_hbm.1, f32[1,1024]{1,0:T(1,128)} %bitcast.5), custom_call_target="tpu_custom_call" | custom-call | flops 6442450944 | bytes 6291456 | tf_op jit(solution)/shard_map/pool/pallas_call | solution.py:247
  17.6 8.0 %all-to-all-start = ((bf16[8,4,1152]{2,1,0:T(4,128)(2,1)}), bf16[8,4,1152]{2,1,0:T(4,128)(2,1)S(1)}, u32[]{:S(2)}, u32[]{:S(2)}) async-start(bf16[8,4,1152]{2,1,0:T(4,128)(2,1)} %pool.1), calls=%async_computation | async-start | bytes 147456 | tf_op jit(solution)/shard_map/all_to_all | solution.py:470
  25.6 0.0 copy-start
  25.6 2.2 %copy-done = bf16[1024,2048]{1,0:T(8,128)(2,1)S(1)} copy-done((bf16[1024,2048]{1,0:T(8,128)(2,1)S(1)}, bf16[1024,2048]{1,0:T(8,128)(2,1)}, u32[]{:S(2)}) %copy-start) | copy-done | bytes 4194328
  27.8 3.0 %gram.1.gram_ref = bf16[1024,1024]{1,0:T(8,128)(2,1)S(1)} custom-call(bf16[1024,2048]{1,0:T(8,128)(2,1)S(1)} %copy-done), custom_call_target="tpu_custom_call" | custom-call | flops 4294967296 | bytes 4194304 | tf_op jit(solution)/shard_map/gram/pallas_call | solution.py:287
  30.8 2.2 %all-to-all-done = bf16[8,4,1152]{2,1,0:T(4,128)(2,1)S(1)} async-done(((bf16[8,4,1152]{2,1,0:T(4,128)(2,1)}), bf16[8,4,1152]{2,1,0:T(4,128)(2,1)S(1)}, u32[]{:S(2)}, u32[]{:S(2)}) %all-to-all-start) | async-done | bytes 73760 | tf_op jit(solution)/shard_map/all_to_all | solution.py:470
  33.0 0.1 broadcast_in_dim.3
  33.1 23.2 %all_to_all.10 = bf16[16,32,1152]{2,1,0:T(8,128)(2,1)S(1)} all-to-all(bf16[16,32,1152]{2,1,0:T(8,128)(2,1)S(1)} %broadcast_in_dim.3), channel_id=1, replica_groups=mesh['dp_0'=8,'dp_1'=4,'dp_2'=4,'dp_3'=2] {'dp_1','dp_2'}, dimensions={0} | all-to-all | bytes 2359296 | tf_op jit(solution)/shard_map/all_to_all | solution.py:474
  56.3 3.6 %collective-permute-start = (bf16[512,1152]{1,0:T(8,128)(2,1)S(1)}, bf16[512,1152]{1,0:T(8,128)(2,1)S(1)}, u32[]{:S(2)}, u32[]{:S(2)}) collective-permute-start(bf16[512,1152]{1,0:T(8,128)(2,1)S(1)} %bitcast.2), channel_id=1, source_target_pairs={{0,1},{1,0},{2,3},{3,2},{4,5},{5,4},{6,7},{7,6},{8,9},{9,8},{10,11... | collective-permute-start | bytes 3538952 | tf_op jit(solution)/shard_map/ppermute | solution.py:476
  59.8 1.5 %sides.1 = (bf16[512,1024]{1,0:T(8,128)(2,1)S(1)}, bf16[512,1024]{1,0:T(8,128)(2,1)S(1)}, f32[512,128]{1,0:T(8,128)S(1)}) custom-call(bf16[512,1152]{1,0:T(8,128)(2,1)S(1)} %bitcast.3, bf16[1024,1024]{1,0:T(8,128)(2,1)S(1)} %gram.1.gram_ref), custom_call_target="tpu_custom_call" | custom-call | flops 1073741824 | bytes 4194304 | tf_op jit(solution)/shard_map/sides/pallas_call | solution.py:322
  61.4 0.9 %collective-permute-done.other_ref = bf16[512,1152]{1,0:T(8,128)(2,1)S(1)} collective-permute-done((bf16[512,1152]{1,0:T(8,128)(2,1)S(1)}, bf16[512,1152]{1,0:T(8,128)(2,1)S(1)}, u32[]{:S(2)}, u32[]{:S(2)}) %collective-permute-start) | collective-permute-done | bytes 1179680 | tf_op jit(solution)/shard_map/ppermute | solution.py:476
  62.3 5.2 %loss.1 = (f32[4]{0:T(128)}, f32[4,1024]{1,0:T(4,128)}) custom-call(bf16[512,1152]{1,0:T(8,128)(2,1)S(1)} %bitcast.4, bf16[512,1152]{1,0:T(8,128)(2,1)S(1)} %collective-permute-done.other_ref, bf16[1024,1024]{1,0:T(8,128)(2,1)S(1)} %gram.1.gram_ref, bf16[512,1024]{1,0:T(8,128)(2,1)S(1)} %get-tuple-element.13.own_left_ref, ...), custom_call_target="tpu_custom_call" | custom-call | flops 4294967296 | bytes 4194304 | tf_op jit(solution)/shard_map/loss/pallas_call | solution.py:437
  (1 shorter events, 0.0 us)
Async XLA Ops:
  17.6 15.3 %all-to-all-start = ((bf16[8,4,1152]{2,1,0:T(4,128)(2,1)}), bf16[8,4,1152]{2,1,0:T(4,128)(2,1)S(1)}, u32[]{:S(2)}, u32[]{:S(2)}) async-start(bf16[8,4,1152]{2,1,0:T(4,128)(2,1)} %pool.1), calls=%async_computation | async-start | bytes 147456 | tf_op jit(solution)/shard_map/all_to_all | solution.py:470
  25.6 2.2 %copy-start = (bf16[1024,2048]{1,0:T(8,128)(2,1)S(1)}, bf16[1024,2048]{1,0:T(8,128)(2,1)}, u32[]{:S(2)}) copy-start(bf16[1024,2048]{1,0:T(8,128)(2,1)} %w_ref) | copy-start | bytes 12582916
  56.3 6.0 %collective-permute-start = (bf16[512,1152]{1,0:T(8,128)(2,1)S(1)}, bf16[512,1152]{1,0:T(8,128)(2,1)S(1)}, u32[]{:S(2)}, u32[]{:S(2)}) collective-permute-start(bf16[512,1152]{1,0:T(8,128)(2,1)S(1)} %bitcast.2), channel_id=1, source_target_pairs={{0,1},{1,0},{2,3},{3,2},{4,5},{5,4},{6,7},{7,6},{8,9},{9,8},{10,11... | collective-permute-start | bytes 3538952 | tf_op jit(solution)/shard_map/ppermute | solution.py:476

commit v6 on v5

--- a/solution.py
+++ b/solution.py
@@ -105,16 +105,17 @@
     k_mark = jnp.where(mine | (feature >= slots), 0.0, FAR).astype(BF16)
     first_half = lane < HEAD_DIM
 
-    def project(kind, some, g, carry):
-        c0 = pl.multiple_of(kind * hidden + g * chunk, chunk)
-        part = dot(x_ref[some, :], wqkv_ref[:, pl.ds(c0, chunk)])
+    def product(kind, some):
+        return dot(x_ref[some, :], wqkv_ref[:, kind * hidden : (kind + 1) * hidden])
+
+    def place(kind, some, part):
         if kind == 0:
             part = part * (LOG2E * HEAD_DIM**-0.5)
         part = part.astype(BF16)
         left = first_half[some]
-        for p in range(chunk // (2 * HEAD_DIM)):
+        for p in range(PAIRS):
             pair = part[:, p * 2 * HEAD_DIM : (p + 1) * 2 * HEAD_DIM]
-            head = g * (chunk // HEAD_DIM) + 2 * p
+            head = 2 * p
             if kind == 0:
                 q_ref[head, some, :] = jnp.where(left, pair, q_mark[some])
                 q_ref[head + 1, some, :] = jnp.where(left, q_mark[some], pair)
@@ -126,16 +127,23 @@
                 for i in range(2):
                     v_ref[head + i, 0:HEAD_DIM, some] = turned[i * HEAD_DIM : (i + 1) * HEAD_DIM]
                     v_ref[head + i, HEAD_DIM:, some] = jnp.ones((ONES, turned.shape[1]), BF16)
-        return carry
-
+
+    def in_turn(steps):
+        ahead = product(*steps[0])
+        for i, step in enumerate(steps):
+            part = ahead
+            if i + 1 < len(steps):
+                ahead = product(*steps[i + 1])
+            place(*step, part)
+
+    pieces = [slice(r * rows // parts, (r + 1) * rows // parts) for r in range(parts)]
     w_copies[0].wait()
     for r in range(parts):
         x_copies[r].wait()
-        project(0, slice(r * rows // parts, (r + 1) * rows // parts), 0, 0)
-    for kind in (1, 2):
-        w_copies[kind].wait()
-        for r in range(parts):
-            project(kind, slice(r * rows // parts, (r + 1) * rows // parts), 0, 0)
+        in_turn([(0, pieces[r])])
+    w_copies[1].wait()
+    w_copies[2].wait()
+    in_turn([(kind, some) for kind in (1, 2) for some in pieces])
 
     wout_copy.wait()
     sums_ref[...] = jnp.zeros_like(sums_ref)
@@ -297,8 +305,59 @@
     )(w_proj)
 
 
-def side_kernel(pooled_ref, gram_ref, left_ref, right_ref, norm_ref, *, block):
+def live_spread(meta):
+    pick = lax.broadcasted_iota(jnp.int32, (META, 128), 0) == 2
+    return dot(meta, pick.astype(F32).astype(BF16))
+
+
+def column_sums(logit, live, shift):
+    rows, columns = logit.shape
+    pieces = []
+    for c in range(0, columns, 128):
+        term = jnp.exp2(logit[:, c : c + 128]) * live
+        if shift is not None and shift <= c < shift + rows:
+            row = lax.broadcasted_iota(jnp.int32, (rows, 128), 0) + shift
+            col = lax.broadcasted_iota(jnp.int32, (rows, 128), 1) + c
+            term = jnp.where(row == col, 0.0, term)
+        pieces.append(jnp.sum(term.reshape(rows // 8, 8, 128), axis=0))
+    return jnp.concatenate(pieces, axis=1)
+
+
+def own_place(slots):
+    z, y, x, _ = (lax.axis_index(a) for a in AXES)
+    begin = ((y * 4 + x) * 8 + z) * slots
+    return begin, pl.multiple_of(begin // 16 * 16, 16)
+
+
+def side_kernel(
+    pooled_ref,
+    gram_ref,
+    left_ref,
+    right_ref,
+    norm_ref,
+    line_ref,
+    own_logit_ref,
+    logit_ref,
+    *,
+    slots,
+    block,
+):
+    part, width = left_ref.shape
     sides(pooled_ref, gram_ref[...], left_ref, right_ref, norm_ref, 0, block)
+    live = live_spread(pooled_ref[:, width:])
+    right = right_ref[...]
+    sums = jnp.zeros((8, part), F32)
+    for b in range(0, part, block):
+        rows = slice(b, b + block)
+        logit = dot_nt(left_ref[rows, :], right)
+        logit_ref[rows, :] = logit
+        sums = sums + column_sums(logit, live[rows], b)
+    row = lax.broadcasted_iota(jnp.int32, (8, part), 0)
+    norms = norm_ref[...].T[0:1]
+    sums = jnp.sum(sums, axis=0, keepdims=True)
+    line_ref[...] = jnp.where(row == 0, sums, jnp.where(row == 1, norms, 0.0))
+    _, base = own_place(slots)
+    own_logit_ref[...] = logit_ref[pl.ds(base, 16), :]
 
 
 def sides(pooled_ref, gram, left_ref, right_ref, norm_ref, place, block):
@@ -315,24 +374,27 @@
         norm_ref[rows, :] = jnp.broadcast_to(rnorm, (block, norm_ref.shape[1]))
 
 
-def own_sides(mine, gram):
+def own_sides(mine, gram, slots):
     part = mine.shape[0]
     width = gram.shape[0]
     vmem = pl.BlockSpec(memory_space=pltpu.VMEM)
     return pl.pallas_call(
-        functools.partial(side_kernel, block=256),
+        functools.partial(side_kernel, slots=slots, block=256),
         out_shape=(
             jax.ShapeDtypeStruct((part, width), BF16),
             jax.ShapeDtypeStruct((part, width), BF16),
             jax.ShapeDtypeStruct((part, 128), F32),
+            jax.ShapeDtypeStruct((8, part), F32),
+            jax.ShapeDtypeStruct((16, part), F32),
         ),
         in_specs=[vmem, vmem],
-        out_specs=(vmem, vmem, vmem),
+        out_specs=(vmem,) * 5,
+        scratch_shapes=[pltpu.VMEM((part, part), F32)],
         compiler_params=pltpu.CompilerParams(vmem_limit_bytes=SIDE_VMEM),
         cost_estimate=pl.CostEstimate(
-            flops=2 * part * width * width,
+            flops=2 * part * width * (width + part),
             bytes_accessed=8 * part * width,
-            transcendentals=part,
+            transcendentals=part * part,
         ),
         name="sides",
     )(mine, gram)
@@ -345,52 +407,43 @@
     own_left_ref,
     own_right_ref,
     own_norm_ref,
+    own_line_ref,
+    own_logit_ref,
+    far_line_ref,
     loss_ref,
     grad_ref,
-    left_ref,
-    right_ref,
     logit_ref,
-    norm_ref,
 ):
-    total, width = right_ref.shape
-    part = total // 2
+    part, width = own_right_ref.shape
     slots = grad_ref.shape[0]
     block = 256
-    gram = gram_ref[...]
-
-    right_ref[0:part, :] = own_right_ref[...]
-    sides(other_ref, gram, left_ref, right_ref, norm_ref, part, block)
 
     meta = jnp.concatenate([mine_ref[:, width:], other_ref[:, width:]], axis=0)
     pick = lax.broadcasted_iota(jnp.int32, (16, META), 0) == lax.broadcasted_iota(
         jnp.int32, (16, META), 1
     )
     lines = dot_nt(pick.astype(F32).astype(BF16), meta)
-    spread = (lax.broadcasted_iota(jnp.int32, (META, 128), 0) == 2).astype(F32).astype(BF16)
-    live_col = dot(meta, spread)
-
-    right = right_ref[...]
-    sums = jnp.zeros((8, total), F32)
-    for b in range(total // block):
-        rows = slice(b * block, (b + 1) * block)
-        left = own_left_ref[rows, :] if b * block < part else left_ref[rows, :]
-        logit = dot_nt(left, right)
+    live = live_spread(mine_ref[:, width:])
+
+    far = other_ref[:, 0:width]
+    far_norm = far_line_ref[1:2, :]
+    spread_norm = jnp.broadcast_to(far_norm, (block, part))
+    far_live = jnp.broadcast_to(lines[2:3, part:], (block, part))
+    far_sums = jnp.zeros((8, part), F32)
+    row_sums = []
+    raws = [dot_nt(own_left_ref[b : b + block, :], far) for b in range(0, part, block)]
+    for i, raw in enumerate(raws):
+        rows = slice(i * block, (i + 1) * block)
+        logit = raw * spread_norm
         logit_ref[rows, :] = logit
-        live = live_col[rows, :]
-        pieces = []
-        for c in range(total // 128):
-            term = jnp.exp2(logit[:, c * 128 : (c + 1) * 128]) * live
-            if b * block <= c * 128 < (b + 1) * block:
-                row = lax.broadcasted_iota(jnp.int32, (block, 128), 0) + b * block
-                col = lax.broadcasted_iota(jnp.int32, (block, 128), 1) + c * 128
-                term = jnp.where(row == col, 0.0, term)
-            pieces.append(jnp.sum(term.reshape(block // 8, 8, 128), axis=0))
-        sums = sums + jnp.concatenate(pieces, axis=1)
-    denominator_line = jnp.sum(sums, axis=0, keepdims=True)
-
-    z, y, x, _ = (lax.axis_index(a) for a in AXES)
-    begin = ((y * 4 + x) * 8 + z) * slots
-    base = pl.multiple_of(begin // 16 * 16, 16)
+        far_sums = far_sums + column_sums(logit, live[rows], None)
+        row = jnp.sum(jnp.exp2(logit) * far_live, axis=1, keepdims=True)
+        row_sums.append(jnp.broadcast_to(row, (block, 128)))
+    own_line = own_line_ref[0:1, :] + jnp.concatenate(row_sums, axis=0).T[0:1]
+    far_line = far_line_ref[0:1, :] + jnp.sum(far_sums, axis=0, keepdims=True)
+    denominator_line = jnp.concatenate([own_line, far_line], axis=1)
+
+    begin, base = own_place(slots)
     within = begin - base
     own_meta = mine_ref[pl.ds(base, 16), width:].astype(F32)
     own_positive = own_meta[:, 0:1] * 32.0 + own_meta[:, 1:2]
@@ -400,7 +453,7 @@
     live_line = lines[2:3, :] > 0.5
     slot_line = lines[3:4, :] * 32.0 + lines[4:5, :]
 
-    logit = logit_ref[pl.ds(base, 16), :]
+    logit = jnp.concatenate([own_logit_ref[...], logit_ref[pl.ds(base, 16), :]], axis=1)
     same = slot_line == own_slot
     raw = jnp.where(same, 0.0, jnp.exp2(logit))
     as_query = jnp.where(live_line, raw, 0.0)
@@ -416,9 +469,10 @@
     key_weights = jnp.where(
         live_line, jnp.where(own_live, raw, 0.0) / denominator_line - hits, 0.0
     )
-    weights = (query_weights + key_weights).astype(BF16)
-    mix = dot(weights, right)
-    image = dot(mix.astype(BF16), gram) * LOGIT_SCALE
+    weights = query_weights + key_weights
+    mix = dot(weights[:, 0:part].astype(BF16), own_right_ref[...])
+    mix = mix + dot((weights[:, part:] * far_norm).astype(BF16), far)
+    image = dot(mix.astype(BF16), gram_ref[...]) * LOGIT_SCALE
     unit_image = own_left_ref[pl.ds(base, 16), :].astype(F32) * (1.0 / (LOGIT_SCALE * LOG2E))
     radial = LOGIT_SCALE * jnp.sum(mix * unit_image, axis=1, keepdims=True)
     rnorm = own_norm_ref[pl.ds(base, 16), 0:1]
@@ -429,10 +483,9 @@
     grad_ref[...] = out
 
 
-def loss_and_grad(mine, other, gram, own, slots):
+def loss_and_grad(mine, other, gram, own, far_line, slots):
     part, padded = mine.shape
     width = padded - META
-    total = 2 * part
     vmem = pl.BlockSpec(memory_space=pltpu.VMEM)
     return pl.pallas_call(
         loss_kernel,
@@ -440,22 +493,17 @@
             jax.ShapeDtypeStruct((slots,), F32),
             jax.ShapeDtypeStruct((slots, width), F32),
         ),
-        in_specs=[vmem] * 6,
+        in_specs=[vmem] * 9,
         out_specs=(pl.BlockSpec(memory_space=pltpu.SMEM), vmem),
-        scratch_shapes=[
-            pltpu.VMEM((total, width), BF16),
-            pltpu.VMEM((total, width), BF16),
-            pltpu.VMEM((total, total), F32),
-            pltpu.VMEM((total, 128), F32),
-        ],
+        scratch_shapes=[pltpu.VMEM((part, part), F32)],
         compiler_params=pltpu.CompilerParams(vmem_limit_bytes=LOSS_VMEM),
         cost_estimate=pl.CostEstimate(
-            flops=4 * total * total * width,
-            bytes_accessed=4 * total * width,
-            transcendentals=total * total,
+            flops=2 * part * part * width,
+            bytes_accessed=8 * part * width,
+            transcendentals=part * part,
         ),
         name="loss",
-    )(mine, other, gram, *own)
+    )(mine, other, gram, *own, far_line)
 
 
 def body(tokens, seg_ids, counts, positives, w_qkv, w_out, ln_gain, w_proj):
@@ -473,9 +521,11 @@
     copies = jnp.broadcast_to(line, (plane_size, *line.shape))
     mine = lax.all_to_all(copies, plane, split_axis=0, concat_axis=0, tiled=True)
     mine = mine.reshape(plane_size * z_size * slots, padded)
-    other = lax.ppermute(mine, "dp_3", [(0, 1), (1, 0)])
-    own = own_sides(mine, gram)
-    return loss_and_grad(mine, other, gram, own, slots)
+    pairs = [(0, 1), (1, 0)]
+    other = lax.ppermute(mine, "dp_3", pairs)
+    own = own_sides(mine, gram, slots)
+    far_line = lax.ppermute(own[3], "dp_3", pairs)
+    return loss_and_grad(mine, other, gram, own, far_line, slots)
 
 
 def solution(mesh):

time: 67.8 us -> 65.7 us (0.969)
  Pallas kernels: 26.7 us -> 24.2 us
    pallas_call x1, Pallas kernels: 5.17 us -> 2.2 us  [loss_and_grad(): pl.pallas_call(loss_kernel, out_shape=(jax.ShapeDtypeStruct((slots,), F32...]
    pallas_call x1, Pallas kernels: 1.53 us -> 2.29 us  [own_sides(): pl.pallas_call(functools.partial(side_kernel, slots=slots, block=256), ou...]
    ppermute x1 -> x2, starting transfers between devices: 3.57 us -> 3.55 us  [the longest x1 3.46 us: body(): other = lax.ppermute(mine, 'dp_3', pairs)]
  transfers between devices with their start and end apart: 2 -> 3, of which waited for: 2 -> 2; matrix products, arithmetic and copies ran while one was open for 0% -> 0% of each run, Pallas kernels for 7% -> 8%
where the time goes in v6:
time: 65.7 us
  Pallas kernels  24.2 us (37%)
  blocking collectives  23.5 us (36%)
  starting transfers between devices  11.5 us (18%)
  waiting for transfers between devices  3.35 us (5%)
  local copies, waits for them, and re-layouts  2.29 us (3%)
  between operations  0.86 us (1%)
    all_to_all x1, blocking collectives, body(): lax.all_to_all(copies, plane, split_axis=0, concat_axis=0, tiled=True)  23.5 us
    pallas_call x1, Pallas kernels, pooled_rows(): pl.pallas_call(functools.partial(pool_kernel, copies=copies, tile=tile),...  16.8 us
    all_to_all x1, starting transfers between devices, body(): lax.all_to_all(packed, 'dp_0', split_axis=0, concat_axis=0, tiled=True)  7.9 us
    ppermute x1, starting transfers between devices, body(): other = lax.ppermute(mine, 'dp_3', pairs)  3.46 us
    pallas_call x1, Pallas kernels, gram_of(): pl.pallas_call(functools.partial(gram_kernel, block=256), out_shape=jax.S...  2.96 us
    pallas_call x1, Pallas kernels, own_sides(): pl.pallas_call(functools.partial(side_kernel, slots=slots, block=256), ou...  2.29 us
    pallas_call x1, Pallas kernels, loss_and_grad(): pl.pallas_call(loss_kernel, out_shape=(jax.ShapeDtypeStruct((slots,), F32...  2.2 us
    unnamed x2, local copies, waits for them, and re-layouts  2.18 us
  transfers between devices with their start and end apart: 3, of which 2 were waited for; matrix products, arithmetic and copies ran while one was open for 0% of the time, Pallas kernels for 8%

profile of v6, /device:TPU:1, one launch (start us, length us, event | category | flops | bytes accessed | tf_op | source)
XLA Modules:
  0.0 65.7 jit_solution(9199717576247167861)
XLA Ops:
  0.6 16.8 %pool.1 = bf16[8,4,1152]{2,1,0:T(4,128)(2,1)} custom-call(s32[1,1024]{1,0:T(1,128)} %seg_ref.1, s32[256]{0:T(256)} %counts_ref.1, s32[4]{0:T(128)} %positives_ref.1, bf16[1024,1024]{1,0:T(8,128)(2,1)} %x_hbm.1, bf16[1024,1536]{1,0:T(8,128)(2,1)} %wqkv_hbm.1, bf16[512,1024]{1,0:T(8,128)(2,1)} %wout_hbm.1, f32[1,1024]{1,0:T(1,128)} %bitcast.5), custom_call_target="tpu_custom_call" | custom-call | flops 6442450944 | bytes 6291456 | tf_op jit(solution)/shard_map/pool/pallas_call | solution.py:255
  17.4 7.9 %all-to-all-start = ((bf16[8,4,1152]{2,1,0:T(4,128)(2,1)}), bf16[8,4,1152]{2,1,0:T(4,128)(2,1)S(1)}, u32[]{:S(2)}, u32[]{:S(2)}) async-start(bf16[8,4,1152]{2,1,0:T(4,128)(2,1)} %pool.1), calls=%async_computation | async-start | bytes 147456 | tf_op jit(solution)/shard_map/all_to_all | solution.py:518
  25.3 0.0 copy-start
  25.3 2.2 %copy-done = bf16[1024,2048]{1,0:T(8,128)(2,1)S(1)} copy-done((bf16[1024,2048]{1,0:T(8,128)(2,1)S(1)}, bf16[1024,2048]{1,0:T(8,128)(2,1)}, u32[]{:S(2)}) %copy-start) | copy-done | bytes 4194328
  27.5 3.0 %gram.1.gram_ref = bf16[1024,1024]{1,0:T(8,128)(2,1)S(1)} custom-call(bf16[1024,2048]{1,0:T(8,128)(2,1)S(1)} %copy-done), custom_call_target="tpu_custom_call" | custom-call | flops 4294967296 | bytes 4194304 | tf_op jit(solution)/shard_map/gram/pallas_call | solution.py:295
  30.5 2.2 %all-to-all-done = bf16[8,4,1152]{2,1,0:T(4,128)(2,1)S(1)} async-done(((bf16[8,4,1152]{2,1,0:T(4,128)(2,1)}), bf16[8,4,1152]{2,1,0:T(4,128)(2,1)S(1)}, u32[]{:S(2)}, u32[]{:S(2)}) %all-to-all-start) | async-done | bytes 73760 | tf_op jit(solution)/shard_map/all_to_all | solution.py:518
  32.7 0.1 broadcast_in_dim.3
  32.8 23.5 %all_to_all.10 = bf16[16,32,1152]{2,1,0:T(8,128)(2,1)S(1)} all-to-all(bf16[16,32,1152]{2,1,0:T(8,128)(2,1)S(1)} %broadcast_in_dim.3), channel_id=1, replica_groups=mesh['dp_0'=8,'dp_1'=4,'dp_2'=4,'dp_3'=2] {'dp_1','dp_2'}, dimensions={0} | all-to-all | bytes 2359296 | tf_op jit(solution)/shard_map/all_to_all | solution.py:522
  56.3 3.5 %collective-permute-start = (bf16[512,1152]{1,0:T(8,128)(2,1)S(1)}, bf16[512,1152]{1,0:T(8,128)(2,1)S(1)}, u32[]{:S(2)}, u32[]{:S(2)}) collective-permute-start(bf16[512,1152]{1,0:T(8,128)(2,1)S(1)} %bitcast.2), channel_id=1, source_target_pairs={{0,1},{1,0},{2,3},{3,2},{4,5},{5,4},{6,7},{7,6},{8,9},{9,8},{10,11... | collective-permute-start | bytes 3538952 | tf_op jit(solution)/shard_map/ppermute | solution.py:525
  59.7 2.3 %sides.1 = (bf16[512,1024]{1,0:T(8,128)(2,1)S(1)}, bf16[512,1024]{1,0:T(8,128)(2,1)S(1)}, f32[512,128]{1,0:T(8,128)S(1)}, f32[8,512]{1,0:T(8,128)S(1)}, f32[16,512]{1,0:T(8,128)S(1)}) custom-call(bf16[512,1152]{1,0:T(8,128)(2,1)S(1)} %bitcast.3, bf16[1024,1024]{1,0:T(8,128)(2,1)S(1)} %gram.1.gram_ref), custom_call_target="tpu_custom_call" | custom-call | flops 1610612736 | bytes 4194304 | tf_op jit(solution)/shard_map/sides/pallas_call | solution.py:381
  62.0 0.1 collective-permute-start.1
  62.1 1.2 %collective-permute-done.1.far_line_ref = f32[8,512]{1,0:T(8,128)S(1)} collective-permute-done((f32[8,512]{1,0:T(8,128)S(1)}, f32[8,512]{1,0:T(8,128)S(1)}, u32[]{:S(2)}, u32[]{:S(2)}) %collective-permute-start.1) | collective-permute-done | bytes 16416 | tf_op jit(solution)/shard_map/ppermute | solution.py:527
  63.3 0.0 collective-permute-done.other_ref
  63.3 2.2 %loss.1 = (f32[4]{0:T(128)}, f32[4,1024]{1,0:T(4,128)}) custom-call(bf16[512,1152]{1,0:T(8,128)(2,1)S(1)} %bitcast.4, bf16[512,1152]{1,0:T(8,128)(2,1)S(1)} %collective-permute-done.other_ref, bf16[1024,1024]{1,0:T(8,128)(2,1)S(1)} %gram.1.gram_ref, bf16[512,1024]{1,0:T(8,128)(2,1)S(1)} %get-tuple-element.15.own_left_ref, ...), custom_call_target="tpu_custom_call" | custom-call | flops 536870912 | bytes 4194304 | tf_op jit(solution)/shard_map/loss/pallas_call | solution.py:490
  (1 shorter events, 0.0 us)
Async XLA Ops:
  17.4 15.2 %all-to-all-start = ((bf16[8,4,1152]{2,1,0:T(4,128)(2,1)}), bf16[8,4,1152]{2,1,0:T(4,128)(2,1)S(1)}, u32[]{:S(2)}, u32[]{:S(2)}) async-start(bf16[8,4,1152]{2,1,0:T(4,128)(2,1)} %pool.1), calls=%async_computation | async-start | bytes 147456 | tf_op jit(solution)/shard_map/all_to_all | solution.py:518
  25.3 2.2 %copy-start = (bf16[1024,2048]{1,0:T(8,128)(2,1)S(1)}, bf16[1024,2048]{1,0:T(8,128)(2,1)}, u32[]{:S(2)}) copy-start(bf16[1024,2048]{1,0:T(8,128)(2,1)} %w_ref) | copy-start | bytes 12582916
  56.3 7.0 %collective-permute-start = (bf16[512,1152]{1,0:T(8,128)(2,1)S(1)}, bf16[512,1152]{1,0:T(8,128)(2,1)S(1)}, u32[]{:S(2)}, u32[]{:S(2)}) collective-permute-start(bf16[512,1152]{1,0:T(8,128)(2,1)S(1)} %bitcast.2), channel_id=1, source_target_pairs={{0,1},{1,0},{2,3},{3,2},{4,5},{5,4},{6,7},{7,6},{8,9},{9,8},{10,11... | collective-permute-start | bytes 3538952 | tf_op jit(solution)/shard_map/ppermute | solution.py:525
  62.0 1.3 %collective-permute-start.1 = (f32[8,512]{1,0:T(8,128)S(1)}, f32[8,512]{1,0:T(8,128)S(1)}, u32[]{:S(2)}, u32[]{:S(2)}) collective-permute-start(f32[8,512]{1,0:T(8,128)S(1)} %get-tuple-element.18.own_line_ref), channel_id=1, source_target_pairs={{0,1},{1,0},{2,3},{3,2},{4,5},{5,4},{6,7},{7,6},{8,9},{9,8},{10,11... | collective-permute-start | bytes 49160 | tf_op jit(solution)/shard_map/ppermute | solution.py:527

commit v7 on v6

--- a/solution.py
+++ b/solution.py
@@ -22,7 +22,7 @@
 F32 = jnp.float32
 POOL_VMEM = 60 * 1024 * 1024
 LOSS_VMEM = 24 * 1024 * 1024
-GRAM_VMEM = 12 * 1024 * 1024
+GRAM_VMEM = 57 * 1024 * 1024
 SIDE_VMEM = 12 * 1024 * 1024
 
 
@@ -278,8 +278,15 @@
     )(seg_ids, counts, positives, tokens, w_qkv, w_out, ln_gain.reshape(1, width))
 
 
-def gram_kernel(w_ref, out_ref, *, block):
-    for b in range(out_ref.shape[0] // block):
+def gram_kernel(w_hbm, out_ref, w_ref, sems, *, block):
+    blocks = out_ref.shape[0] // block
+    copies = []
+    for b in range(blocks):
+        part = slice(b * block, (b + 1) * block)
+        copies.append(pltpu.make_async_copy(w_hbm.at[part, :], w_ref.at[part, :], sems.at[b]))
+        copies[-1].start()
+    for b in range(blocks):
+        copies[b].wait()
         right = w_ref[b * block : (b + 1) * block, :]
         for c in range(b + 1):
             left = w_ref[c * block : (c + 1) * block, :]
@@ -291,12 +298,16 @@
 
 def gram_of(w_proj):
     rows, depth = w_proj.shape
-    vmem = pl.BlockSpec(memory_space=pltpu.VMEM)
+    block = 256
     return pl.pallas_call(
-        functools.partial(gram_kernel, block=256),
+        functools.partial(gram_kernel, block=block),
         out_shape=jax.ShapeDtypeStruct((rows, rows), BF16),
-        in_specs=[vmem],
-        out_specs=vmem,
+        in_specs=[pl.BlockSpec(memory_space=pltpu.HBM)],
+        out_specs=pl.BlockSpec(memory_space=pltpu.VMEM),
+        scratch_shapes=[
+            pltpu.VMEM((rows, depth), BF16),
+            pltpu.SemaphoreType.DMA((rows // block,)),
+        ],
         compiler_params=pltpu.CompilerParams(vmem_limit_bytes=GRAM_VMEM),
         cost_estimate=pl.CostEstimate(
             flops=2 * rows * rows * depth, bytes_accessed=2 * rows * depth, transcendentals=0

time: 65.7 us -> 66 us (level)
  Pallas kernels: 24.2 us -> 27.4 us
  local copies, waits for them, and re-layouts: 2.29 us -> 0.11 us
  waiting for transfers between devices: 3.35 us -> 1.77 us
    pallas_call x1, Pallas kernels: 2.96 us -> 6.76 us  [gram_of(): pl.pallas_call(functools.partial(gram_kernel, block=block), out_shape=jax...]
    unnamed x2, local copies, waits for them, and re-layouts: 2.18 us -> 0.01 us
    all_to_all x1, waiting for transfers between devices: 2.18 us -> 0.59 us  [body(): lax.all_to_all(packed, 'dp_0', split_axis=0, concat_axis=0, tiled=True)]
    all_to_all x1, starting transfers between devices: 7.9 us -> 8.98 us  [body(): lax.all_to_all(packed, 'dp_0', split_axis=0, concat_axis=0, tiled=True)]
  transfers between devices with their start and end apart: 3 -> 3, of which waited for: 2 -> 2; matrix products, arithmetic and copies ran while one was open for 0% -> 0% of each run, Pallas kernels for 8% -> 14%
where the time goes in v7:
time: 66 us; the launch traced here: 65.6 us
  Pallas kernels  27.4 us (42%)
  blocking collectives  23.4 us (35%)
  starting transfers between devices  12.1 us (18%)
  waiting for transfers between devices  1.77 us (3%)
  between operations  0.86 us (1%)
    all_to_all x1, blocking collectives, body(): lax.all_to_all(copies, plane, split_axis=0, concat_axis=0, tiled=True)  23.4 us
    pallas_call x1, Pallas kernels, pooled_rows(): pl.pallas_call(functools.partial(pool_kernel, copies=copies, tile=tile),...  16.1 us
    all_to_all x1, starting transfers between devices, body(): lax.all_to_all(packed, 'dp_0', split_axis=0, concat_axis=0, tiled=True)  8.98 us
    pallas_call x1, Pallas kernels, gram_of(): pl.pallas_call(functools.partial(gram_kernel, block=block), out_shape=jax...  6.76 us
    ppermute x1, starting transfers between devices, body(): other = lax.ppermute(mine, 'dp_3', pairs)  3.03 us
    pallas_call x1, Pallas kernels, own_sides(): pl.pallas_call(functools.partial(side_kernel, slots=slots, block=256), ou...  2.29 us
    pallas_call x1, Pallas kernels, loss_and_grad(): pl.pallas_call(loss_kernel, out_shape=(jax.ShapeDtypeStruct((slots,), F32...  2.2 us
  transfers between devices with their start and end apart: 3, of which 2 were waited for; matrix products, arithmetic and copies ran while one was open for 0% of the time, Pallas kernels for 14%

profile of v7, /device:TPU:1, one launch (start us, length us, event | category | flops | bytes accessed | tf_op | source)
XLA Modules:
  0.0 65.6 jit_solution(17563982866711347709)
XLA Ops:
  0.6 16.1 %pool.1 = bf16[8,4,1152]{2,1,0:T(4,128)(2,1)} custom-call(s32[1,1024]{1,0:T(1,128)} %seg_ref.1, s32[256]{0:T(256)} %counts_ref.1, s32[4]{0:T(128)} %positives_ref.1, bf16[1024,1024]{1,0:T(8,128)(2,1)} %x_hbm.1, bf16[1024,1536]{1,0:T(8,128)(2,1)} %wqkv_hbm.1, bf16[512,1024]{1,0:T(8,128)(2,1)} %wout_hbm.1, f32[1,1024]{1,0:T(1,128)} %bitcast.5), custom_call_target="tpu_custom_call" | custom-call | flops 6442450944 | bytes 6291456 | tf_op jit(solution)/shard_map/pool/pallas_call | solution.py:255
  16.8 9.0 %all-to-all-start = ((bf16[8,4,1152]{2,1,0:T(4,128)(2,1)}), bf16[8,4,1152]{2,1,0:T(4,128)(2,1)S(1)}, u32[]{:S(2)}, u32[]{:S(2)}) async-start(bf16[8,4,1152]{2,1,0:T(4,128)(2,1)} %pool.1), calls=%async_computation | async-start | bytes 147456 | tf_op jit(solution)/shard_map/all_to_all | solution.py:529
  25.8 6.8 %gram.1.gram_ref = bf16[1024,1024]{1,0:T(8,128)(2,1)} custom-call(bf16[1024,2048]{1,0:T(8,128)(2,1)} %w_hbm), custom_call_target="tpu_custom_call" | custom-call | flops 4294967296 | bytes 4194304 | tf_op jit(solution)/shard_map/gram/pallas_call | solution.py:302
  32.5 0.0 copy-start
  32.5 0.6 all-to-all-done
  33.2 0.1 broadcast_in_dim.3
  33.2 23.4 %all_to_all.10 = bf16[16,32,1152]{2,1,0:T(8,128)(2,1)S(1)} all-to-all(bf16[16,32,1152]{2,1,0:T(8,128)(2,1)S(1)} %broadcast_in_dim.3), channel_id=1, replica_groups=mesh['dp_0'=8,'dp_1'=4,'dp_2'=4,'dp_3'=2] {'dp_1','dp_2'}, dimensions={0} | all-to-all | bytes 2359296 | tf_op jit(solution)/shard_map/all_to_all | solution.py:533
  56.6 3.0 %collective-permute-start = (bf16[512,1152]{1,0:T(8,128)(2,1)S(1)}, bf16[512,1152]{1,0:T(8,128)(2,1)S(1)}, u32[]{:S(2)}, u32[]{:S(2)}) collective-permute-start(bf16[512,1152]{1,0:T(8,128)(2,1)S(1)} %bitcast.2), channel_id=1, source_target_pairs={{0,1},{1,0},{2,3},{3,2},{4,5},{5,4},{6,7},{7,6},{8,9},{9,8},{10,11... | collective-permute-start | bytes 3538952 | tf_op jit(solution)/shard_map/ppermute | solution.py:536
  59.7 0.0 copy-done
  59.7 2.3 %sides.1 = (bf16[512,1024]{1,0:T(8,128)(2,1)S(1)}, bf16[512,1024]{1,0:T(8,128)(2,1)S(1)}, f32[512,128]{1,0:T(8,128)S(1)}, f32[8,512]{1,0:T(8,128)S(1)}, f32[16,512]{1,0:T(8,128)S(1)}) custom-call(bf16[512,1152]{1,0:T(8,128)(2,1)S(1)} %bitcast.3, bf16[1024,1024]{1,0:T(8,128)(2,1)S(1)} %copy-done), custom_call_target="tpu_custom_call" | custom-call | flops 1610612736 | bytes 4194304 | tf_op jit(solution)/shard_map/sides/pallas_call | solution.py:392
  62.0 0.1 collective-permute-start.1
  62.1 1.2 %collective-permute-done.1.far_line_ref = f32[8,512]{1,0:T(8,128)S(1)} collective-permute-done((f32[8,512]{1,0:T(8,128)S(1)}, f32[8,512]{1,0:T(8,128)S(1)}, u32[]{:S(2)}, u32[]{:S(2)}) %collective-permute-start.1) | collective-permute-done | bytes 16416 | tf_op jit(solution)/shard_map/ppermute | solution.py:538
  63.2 0.0 collective-permute-done.other_ref
  63.2 2.2 %loss.1 = (f32[4]{0:T(128)}, f32[4,1024]{1,0:T(4,128)}) custom-call(bf16[512,1152]{1,0:T(8,128)(2,1)S(1)} %bitcast.4, bf16[512,1152]{1,0:T(8,128)(2,1)S(1)} %collective-permute-done.other_ref, bf16[1024,1024]{1,0:T(8,128)(2,1)S(1)} %copy-done, bf16[512,1024]{1,0:T(8,128)(2,1)S(1)} %get-tuple-element.15.own_left_ref, ...), custom_call_target="tpu_custom_call" | custom-call | flops 536870912 | bytes 4194304 | tf_op jit(solution)/shard_map/loss/pallas_call | solution.py:501
  (1 shorter events, 0.0 us)
Async XLA Ops:
  16.8 16.4 %all-to-all-start = ((bf16[8,4,1152]{2,1,0:T(4,128)(2,1)}), bf16[8,4,1152]{2,1,0:T(4,128)(2,1)S(1)}, u32[]{:S(2)}, u32[]{:S(2)}) async-start(bf16[8,4,1152]{2,1,0:T(4,128)(2,1)} %pool.1), calls=%async_computation | async-start | bytes 147456 | tf_op jit(solution)/shard_map/all_to_all | solution.py:529
  32.5 27.1 %copy-start = (bf16[1024,1024]{1,0:T(8,128)(2,1)S(1)}, bf16[1024,1024]{1,0:T(8,128)(2,1)}, u32[]{:S(2)}) copy-start(bf16[1024,1024]{1,0:T(8,128)(2,1)} %gram.1.gram_ref) | copy-start | bytes 6291460
  56.6 6.6 %collective-permute-start = (bf16[512,1152]{1,0:T(8,128)(2,1)S(1)}, bf16[512,1152]{1,0:T(8,128)(2,1)S(1)}, u32[]{:S(2)}, u32[]{:S(2)}) collective-permute-start(bf16[512,1152]{1,0:T(8,128)(2,1)S(1)} %bitcast.2), channel_id=1, source_target_pairs={{0,1},{1,0},{2,3},{3,2},{4,5},{5,4},{6,7},{7,6},{8,9},{9,8},{10,11... | collective-permute-start | bytes 3538952 | tf_op jit(solution)/shard_map/ppermute | solution.py:536
  62.0 1.3 %collective-permute-start.1 = (f32[8,512]{1,0:T(8,128)S(1)}, f32[8,512]{1,0:T(8,128)S(1)}, u32[]{:S(2)}, u32[]{:S(2)}) collective-permute-start(f32[8,512]{1,0:T(8,128)S(1)} %get-tuple-element.18.own_line_ref), channel_id=1, source_target_pairs={{0,1},{1,0},{2,3},{3,2},{4,5},{5,4},{6,7},{7,6},{8,9},{9,8},{10,11... | collective-permute-start | bytes 49160 | tf_op jit(solution)/shard_map/ppermute | solution.py:538

commit v8 on v6

--- a/solution.py
+++ b/solution.py
@@ -400,6 +400,29 @@
     )(mine, gram)
 
 
+def cross_kernel(left_ref, other_ref, raw_ref, *, block):
+    part, width = left_ref.shape
+    far = other_ref[:, 0:width]
+    for b in range(0, part, block):
+        raw_ref[b : b + block, :] = dot_nt(left_ref[b : b + block, :], far)
+
+
+def cross_logits(left, other):
+    part, width = left.shape
+    vmem = pl.BlockSpec(memory_space=pltpu.VMEM)
+    return pl.pallas_call(
+        functools.partial(cross_kernel, block=256),
+        out_shape=jax.ShapeDtypeStruct((part, part), F32),
+        in_specs=[vmem, vmem],
+        out_specs=vmem,
+        compiler_params=pltpu.CompilerParams(vmem_limit_bytes=SIDE_VMEM),
+        cost_estimate=pl.CostEstimate(
+            flops=2 * part * part * width, bytes_accessed=8 * part * width, transcendentals=0
+        ),
+        name="cross",
+    )(left, other)
+
+
 def loss_kernel(
     mine_ref,
     other_ref,
@@ -410,6 +433,7 @@
     own_line_ref,
     own_logit_ref,
     far_line_ref,
+    raw_ref,
     loss_ref,
     grad_ref,
     logit_ref,
@@ -431,7 +455,7 @@
     far_live = jnp.broadcast_to(lines[2:3, part:], (block, part))
     far_sums = jnp.zeros((8, part), F32)
     row_sums = []
-    raws = [dot_nt(own_left_ref[b : b + block, :], far) for b in range(0, part, block)]
+    raws = [raw_ref[b : b + block, :] for b in range(0, part, block)]
     for i, raw in enumerate(raws):
         rows = slice(i * block, (i + 1) * block)
         logit = raw * spread_norm
@@ -483,7 +507,7 @@
     grad_ref[...] = out
 
 
-def loss_and_grad(mine, other, gram, own, far_line, slots):
+def loss_and_grad(mine, other, gram, own, far_line, raw, slots):
     part, padded = mine.shape
     width = padded - META
     vmem = pl.BlockSpec(memory_space=pltpu.VMEM)
@@ -493,7 +517,7 @@
             jax.ShapeDtypeStruct((slots,), F32),
             jax.ShapeDtypeStruct((slots, width), F32),
         ),
-        in_specs=[vmem] * 9,
+        in_specs=[vmem] * 10,
         out_specs=(pl.BlockSpec(memory_space=pltpu.SMEM), vmem),
         scratch_shapes=[pltpu.VMEM((part, part), F32)],
         compiler_params=pltpu.CompilerParams(vmem_limit_bytes=LOSS_VMEM),
@@ -503,7 +527,7 @@
             transcendentals=part * part,
         ),
         name="loss",
-    )(mine, other, gram, *own, far_line)
+    )(mine, other, gram, *own, far_line, raw)
 
 
 def body(tokens, seg_ids, counts, positives, w_qkv, w_out, ln_gain, w_proj):
@@ -525,7 +549,8 @@
     other = lax.ppermute(mine, "dp_3", pairs)
     own = own_sides(mine, gram, slots)
     far_line = lax.ppermute(own[3], "dp_3", pairs)
-    return loss_and_grad(mine, other, gram, own, far_line, slots)
+    raw = cross_logits(own[0], other)
+    return loss_and_grad(mine, other, gram, own, far_line, raw, slots)
 
 
 def solution(mesh):

time: 65.7 us -> 65.3 us (level)
  waiting for transfers between devices: 3.35 us -> 2.69 us
    ppermute x1, waiting for transfers between devices: 1.17 us -> 0.36 us  [body(): far_line = lax.ppermute(own[3], 'dp_3', pairs)]
    pallas_call x0 -> x1, Pallas kernels: none -> 0.73 us  [cross_logits(): pl.pallas_call(functools.partial(cross_kernel, block=256), out_shape=jax....]
  transfers between devices with their start and end apart: 3 -> 3, of which waited for: 2 -> 3; matrix products, arithmetic and copies ran while one was open for 0% -> 0% of each run, Pallas kernels for 8% -> 9%
where the time goes in v8:
time: 65.3 us; the launch traced here: 64.8 us
  Pallas kernels  23.9 us (37%)
  blocking collectives  23.4 us (36%)
  starting transfers between devices  11.7 us (18%)
  waiting for transfers between devices  2.69 us (4%)
  local copies, waits for them, and re-layouts  2.29 us (4%)
  between operations  0.87 us (1%)
    all_to_all x1, blocking collectives, body(): lax.all_to_all(copies, plane, split_axis=0, concat_axis=0, tiled=True)  23.4 us
    pallas_call x1, Pallas kernels, pooled_rows(): pl.pallas_call(functools.partial(pool_kernel, copies=copies, tile=tile),...  16.2 us
    all_to_all x1, starting transfers between devices, body(): lax.all_to_all(packed, 'dp_0', split_axis=0, concat_axis=0, tiled=True)  8.2 us
    ppermute x1, starting transfers between devices, body(): other = lax.ppermute(mine, 'dp_3', pairs)  3.45 us
    pallas_call x1, Pallas kernels, gram_of(): pl.pallas_call(functools.partial(gram_kernel, block=256), out_shape=jax.S...  2.96 us
    pallas_call x1, Pallas kernels, own_sides(): pl.pallas_call(functools.partial(side_kernel, slots=slots, block=256), ou...  2.29 us
    all_to_all x1, waiting for transfers between devices, body(): lax.all_to_all(packed, 'dp_0', split_axis=0, concat_axis=0, tiled=True)  2.26 us
    unnamed x2, local copies, waits for them, and re-layouts  2.18 us
  transfers between devices with their start and end apart: 3, of which 3 were waited for; matrix products, arithmetic and copies ran while one was open for 0% of the time, Pallas kernels for 9%

profile of v8, /device:TPU:1, one launch (start us, length us, event | category | flops | bytes accessed | tf_op | source)
XLA Modules:
  0.0 64.8 jit_solution(17609316114559722838)
XLA Ops:
  0.6 16.2 %pool.1 = bf16[8,4,1152]{2,1,0:T(4,128)(2,1)} custom-call(s32[1,1024]{1,0:T(1,128)} %seg_ref.1, s32[256]{0:T(256)} %counts_ref.1, s32[4]{0:T(128)} %positives_ref.1, bf16[1024,1024]{1,0:T(8,128)(2,1)} %x_hbm.1, bf16[1024,1536]{1,0:T(8,128)(2,1)} %wqkv_hbm.1, bf16[512,1024]{1,0:T(8,128)(2,1)} %wout_hbm.1, f32[1,1024]{1,0:T(1,128)} %bitcast.5), custom_call_target="tpu_custom_call" | custom-call | flops 6442450944 | bytes 6291456 | tf_op jit(solution)/shard_map/pool/pallas_call | solution.py:255
  16.8 8.2 %all-to-all-start = ((bf16[8,4,1152]{2,1,0:T(4,128)(2,1)}), bf16[8,4,1152]{2,1,0:T(4,128)(2,1)S(1)}, u32[]{:S(2)}, u32[]{:S(2)}) async-start(bf16[8,4,1152]{2,1,0:T(4,128)(2,1)} %pool.1), calls=%async_computation | async-start | bytes 147456 | tf_op jit(solution)/shard_map/all_to_all | solution.py:542
  25.0 0.0 copy-start
  25.0 2.2 %copy-done = bf16[1024,2048]{1,0:T(8,128)(2,1)S(1)} copy-done((bf16[1024,2048]{1,0:T(8,128)(2,1)S(1)}, bf16[1024,2048]{1,0:T(8,128)(2,1)}, u32[]{:S(2)}) %copy-start) | copy-done | bytes 4194328
  27.2 3.0 %gram.1.gram_ref = bf16[1024,1024]{1,0:T(8,128)(2,1)S(1)} custom-call(bf16[1024,2048]{1,0:T(8,128)(2,1)S(1)} %copy-done), custom_call_target="tpu_custom_call" | custom-call | flops 4294967296 | bytes 4194304 | tf_op jit(solution)/shard_map/gram/pallas_call | solution.py:295
  30.2 2.3 %all-to-all-done = bf16[8,4,1152]{2,1,0:T(4,128)(2,1)S(1)} async-done(((bf16[8,4,1152]{2,1,0:T(4,128)(2,1)}), bf16[8,4,1152]{2,1,0:T(4,128)(2,1)S(1)}, u32[]{:S(2)}, u32[]{:S(2)}) %all-to-all-start) | async-done | bytes 73760 | tf_op jit(solution)/shard_map/all_to_all | solution.py:542
  32.5 0.1 broadcast_in_dim.3
  32.6 23.4 %all_to_all.10 = bf16[16,32,1152]{2,1,0:T(8,128)(2,1)S(1)} all-to-all(bf16[16,32,1152]{2,1,0:T(8,128)(2,1)S(1)} %broadcast_in_dim.3), channel_id=1, replica_groups=mesh['dp_0'=8,'dp_1'=4,'dp_2'=4,'dp_3'=2] {'dp_1','dp_2'}, dimensions={0} | all-to-all | bytes 2359296 | tf_op jit(solution)/shard_map/all_to_all | solution.py:546
  55.9 3.4 %collective-permute-start = (bf16[512,1152]{1,0:T(8,128)(2,1)S(1)}, bf16[512,1152]{1,0:T(8,128)(2,1)S(1)}, u32[]{:S(2)}, u32[]{:S(2)}) collective-permute-start(bf16[512,1152]{1,0:T(8,128)(2,1)S(1)} %bitcast.2), channel_id=1, source_target_pairs={{0,1},{1,0},{2,3},{3,2},{4,5},{5,4},{6,7},{7,6},{8,9},{9,8},{10,11... | collective-permute-start | bytes 3538952 | tf_op jit(solution)/shard_map/ppermute | solution.py:549
  59.4 2.3 %sides.1 = (bf16[512,1024]{1,0:T(8,128)(2,1)S(1)}, bf16[512,1024]{1,0:T(8,128)(2,1)S(1)}, f32[512,128]{1,0:T(8,128)S(1)}, f32[8,512]{1,0:T(8,128)S(1)}, f32[16,512]{1,0:T(8,128)S(1)}) custom-call(bf16[512,1152]{1,0:T(8,128)(2,1)S(1)} %bitcast.3, bf16[1024,1024]{1,0:T(8,128)(2,1)S(1)} %gram.1.gram_ref), custom_call_target="tpu_custom_call" | custom-call | flops 1610612736 | bytes 4194304 | tf_op jit(solution)/shard_map/sides/pallas_call | solution.py:381
  61.7 0.1 collective-permute-start.1
  61.8 0.1 collective-permute-done.other_ref
  61.8 0.7 %cross.1.raw_ref = f32[512,512]{1,0:T(8,128)S(1)} custom-call(bf16[512,1024]{1,0:T(8,128)(2,1)S(1)} %get-tuple-element.15.left_ref.own_left_ref, bf16[512,1152]{1,0:T(8,128)(2,1)S(1)} %collective-permute-done.other_ref), custom_call_target="tpu_custom_call" | custom-call | flops 536870912 | bytes 4194304 | tf_op jit(solution)/shard_map/cross/pallas_call | solution.py:413
  62.6 0.4 collective-permute-done.1.far_line_ref
  62.9 1.7 %loss.1 = (f32[4]{0:T(128)}, f32[4,1024]{1,0:T(4,128)}) custom-call(bf16[512,1152]{1,0:T(8,128)(2,1)S(1)} %bitcast.4, bf16[512,1152]{1,0:T(8,128)(2,1)S(1)} %collective-permute-done.other_ref, bf16[1024,1024]{1,0:T(8,128)(2,1)S(1)} %gram.1.gram_ref, bf16[512,1024]{1,0:T(8,128)(2,1)S(1)} %get-tuple-element.15.left_ref.own_left_ref, ...), custom_call_target="tpu_custom_call" | custom-call | flops 536870912 | bytes 4194304 | tf_op jit(solution)/shard_map/loss/pallas_call | solution.py:514
  (1 shorter events, 0.0 us)
Async XLA Ops:
  16.8 15.6 %all-to-all-start = ((bf16[8,4,1152]{2,1,0:T(4,128)(2,1)}), bf16[8,4,1152]{2,1,0:T(4,128)(2,1)S(1)}, u32[]{:S(2)}, u32[]{:S(2)}) async-start(bf16[8,4,1152]{2,1,0:T(4,128)(2,1)} %pool.1), calls=%async_computation | async-start | bytes 147456 | tf_op jit(solution)/shard_map/all_to_all | solution.py:542
  25.0 2.2 %copy-start = (bf16[1024,2048]{1,0:T(8,128)(2,1)S(1)}, bf16[1024,2048]{1,0:T(8,128)(2,1)}, u32[]{:S(2)}) copy-start(bf16[1024,2048]{1,0:T(8,128)(2,1)} %w_ref) | copy-start | bytes 12582916
  55.9 5.9 %collective-permute-start = (bf16[512,1152]{1,0:T(8,128)(2,1)S(1)}, bf16[512,1152]{1,0:T(8,128)(2,1)S(1)}, u32[]{:S(2)}, u32[]{:S(2)}) collective-permute-start(bf16[512,1152]{1,0:T(8,128)(2,1)S(1)} %bitcast.2), channel_id=1, source_target_pairs={{0,1},{1,0},{2,3},{3,2},{4,5},{5,4},{6,7},{7,6},{8,9},{9,8},{10,11... | collective-permute-start | bytes 3538952 | tf_op jit(solution)/shard_map/ppermute | solution.py:549
  61.7 1.3 %collective-permute-start.1 = (f32[8,512]{1,0:T(8,128)S(1)}, f32[8,512]{1,0:T(8,128)S(1)}, u32[]{:S(2)}, u32[]{:S(2)}) collective-permute-start(f32[8,512]{1,0:T(8,128)S(1)} %get-tuple-element.18.own_line_ref), channel_id=1, source_target_pairs={{0,1},{1,0},{2,3},{3,2},{4,5},{5,4},{6,7},{7,6},{8,9},{9,8},{10,11... | collective-permute-start | bytes 49160 | tf_op jit(solution)/shard_map/ppermute | solution.py:551
